TPU v7x, 256 devices: a 2x2x32 block of a 4x8x32 slice. The times are simulated.
256 devices in a mesh: grp: 4 (over y, x), seq: 32 (over z), tp: 2 (over core).
Axes of the slice: x: 2, y: 2, z: 32, core: 2. Of those that a mesh axis runs over, the one named last changes fastest.
The devices are a block of a 4x8x32 slice.
Arguments:
- visual_q: bfloat16 [32768, 1536], P(('grp', 'seq'), 'tp'), parts along dimension 0, may hold values from -8 to 8
- visual_key_input: bfloat16 [32768, 1536], P(('grp', 'seq'), 'tp'), parts along dimension 0, may hold values from -8 to 8
- visual_v: bfloat16 [32768, 1536], P(('grp', 'seq'), 'tp'), parts along dimension 0, may hold values from -6 to 6
- text_k: bfloat16 [1024, 1536], P(('grp', 'seq'), 'tp'), parts along dimension 0, may hold values from -6 to 6
- text_v: bfloat16 [1024, 1536], P(('grp', 'seq'), 'tp'), parts along dimension 0, may hold values from -6 to 6
- text_mask: int32 [1024], P(('grp', 'seq')), parts along dimension 0, may hold values from 0 to 1, as said below
- slab_order: int32 [128], P(('grp', 'seq')), parts along dimension 0, may hold values from 0 to 31, each once
- q_gain: float32 [128], replicated, may hold values from 0.8 to 6
- key_norm_gain: float32 [128], replicated, may hold values from 0.8 to 6
- w_out: bfloat16 [1536, 3072], P('tp'), may hold values from -0.8984375 to 0.8984375
Outputs:
- attended: bfloat16 [32768, 3072], P(('grp', 'seq', 'tp')), parts along dimension 0
There are 4 independent parts, one for each index of `grp`. A program takes and returns all parts, laid end to end along the dimension named above; an argument that names none is the same for every part. Nothing has to cross between parts.
Inputs may be any that keep to these rules, and one draw needn't show every extreme that they name: `text_mask`: the first entries are 1 and the rest 0, with at least 32 ones. `slab_order`: each slab number once.
All inputs are finite; a program needn't handle non-finite values.
Results may differ from a plain program's by a relative error of at most 0.013.
The roundings to bfloat16 on the way count: a program that leaves them out, or rounds other values in their place, can miss the bound.
Values may be sent and summed in bfloat16 or wider, within the bound.
No kernel may reach another device: no remote copies, remote signals or barrier semaphores. Data moves between devices by JAX's collectives and lax.ppermute only.
A program may use at most 128 MiB of HBM per device.

v0:
```python
import functools

import jax
import jax.numpy as jnp
import numpy as np
from jax import lax
from jax.experimental import pallas as pl
from jax.experimental.pallas import tpu as pltpu
from jax.sharding import PartitionSpec as P


SLAB_H = 2
WIDE = 32
SPLITS = (32, 48, 48)
HEAD = 128
NEGATIVE = -1e30
PAD = 8


def color_edges(edges, colors):
    at_src, at_dst = {}, {}
    for s, d in edges:
        at_src.setdefault(s, {})
        at_dst.setdefault(d, {})
    for s, d in edges:
        a = next(c for c in range(colors) if c not in at_src[s])
        b = next(c for c in range(colors) if c not in at_dst[d])
        if a != b:
            path = []
            node, side, want = d, 1, a
            while True:
                table = at_dst if side else at_src
                if want not in table[node]:
                    break
                other = table[node][want]
                path.append((other, node, want) if side else (node, other, want))
                node, side, want = other, 1 - side, (b if want == a else a)
            for ps, pd, c in path:
                del at_src[ps][c], at_dst[pd][c]
            for ps, pd, c in path:
                n = b if c == a else a
                at_src[ps][n] = pd
                at_dst[pd][n] = ps
        at_src[s][a] = d
        at_dst[d][a] = s
    return at_src


def sort_rounds(at_src, at_dst, colors, n_tp, cost):
    for _ in range(20):
        moved = False
        for a in range(colors):
            for b in range(a + 1, colors):
                seen = set()
                ends = [(0, n) for n in at_src if (a in at_src[n]) != (b in at_src[n])]
                ends += [(1, n) for n in at_dst if (a in at_dst[n]) != (b in at_dst[n])]
                ends += [(0, n) for n in at_src if a in at_src[n]]
                for start in ends:
                    stack, edges = [start], set()
                    while stack:
                        side, n = stack.pop()
                        if (side, n) in seen:
                            continue
                        seen.add((side, n))
                        table = (at_dst if side else at_src)[n]
                        for c in (a, b):
                            if c in table:
                                edges.add((table[c], n, c) if side else (n, table[c], c))
                                stack.append((1 - side, table[c]))
                    gain = sum(cost(s, d, c) - cost(s, d, a + b - c) for s, d, c in edges)
                    if gain > 1e-6:
                        moved = True
                        for s, d, c in edges:
                            del at_src[s][c], at_dst[d][c]
                        for s, d, c in edges:
                            at_src[s][a + b - c] = d
                            at_dst[d][a + b - c] = s
        for chip in sorted({d // n_tp for d in at_dst}):
            slots = [(d, r) for d in sorted(at_dst) if d // n_tp == chip for r in range(colors)]
            for i in range(len(slots)):
                for j in range(i):
                    (d1, r1), (d2, r2) = slots[i], slots[j]
                    s1, s2 = at_dst[d1][r1], at_dst[d2][r2]
                    if r1 == r2 or s1 == s2 or r2 in at_src[s1] or r1 in at_src[s2]:
                        continue
                    before = cost(s1, d1, r1) + cost(s2, d2, r2)
                    if cost(s1, d2, r2) + cost(s2, d1, r1) < before - 1e-6:
                        moved = True
                        del at_src[s1][r1], at_src[s2][r2]
                        at_src[s1][r2], at_src[s2][r1] = d2, d1
                        at_dst[d1][r1], at_dst[d2][r2] = s2, s1
        if not moved:
            break


def plan(n_seq, n_tp, heads):
    total = heads * n_tp
    chips = 2
    rounds = n_seq // (chips * n_tp)
    owner = {}
    for arc in range(total):
        start = arc * n_seq // total
        tp, local = arc % n_tp, arc // n_tp
        for z in range(n_seq):
            rel = (z - start - 1) % n_seq
            near, chip = (rel, start + 1) if rel < n_seq // 2 else (n_seq - 1 - rel, start)
            owner[(z * n_tp + tp, local)] = chip % n_seq * n_tp + near % n_tp
    at_src = color_edges(sorted((src, dst) for (src, _), dst in owner.items()), rounds)
    at_dst = {}
    for src, table in at_src.items():
        for r, dst in table.items():
            at_dst.setdefault(dst, {})[r] = src

    def hops(src, dst):
        apart = abs(src // n_tp - dst // n_tp)
        return min(apart, n_seq - apart)

    per_round = n_seq / 2 / rounds
    for power in (1, 2, 3, 4):
        sort_rounds(
            at_src, at_dst, rounds, n_tp, lambda s, d, c: abs(hops(s, d) - per_round * (c + 0.25)) ** power
        )
    order = [r for pair in zip(reversed(range(rounds // 2, rounds)), range(rounds // 2)) for r in pair]
    local_of = {}
    for (src, local), dst in owner.items():
        local_of.setdefault((src, dst // n_tp), []).append(local)
    perms = [[] for _ in range(rounds)]
    send = np.zeros((n_seq * n_tp, rounds), np.int32)
    valid = np.zeros((n_seq * n_tp, rounds), np.int32)
    for src in sorted(at_src):
        for r, dst in sorted(at_src[src].items()):
            (local,) = local_of[(src, dst // n_tp)]
            slot = order.index(r)
            perms[slot].append((src, dst))
            send[src, slot] = local
            valid[src, slot] = 1
    cross, flip = [], []
    for arc in range(total):
        start = arc * n_seq // total
        after = (start + 1) % n_seq
        for t in range(n_tp):
            cross += [(start * n_tp + t, after * n_tp + t), (after * n_tp + t, start * n_tp + t)]
            flip += [(chip * n_tp + t, chip * n_tp + (t + 1) % n_tp) for chip in (start, after)]
    return rounds, perms, send, valid, cross, flip


def rope_tables(positions, size):
    half = size // 2
    freq = np.float32(10000.0) ** (-np.arange(half, dtype=np.float32) / np.float32(half))
    angle = np.asarray(positions, np.float32)[:, None] * freq[None, :]
    cos, sin = np.cos(angle), np.sin(angle)
    return np.concatenate([cos, cos], 1), np.concatenate([-sin, sin], 1)


def position_tables(rows, heights):
    local = np.arange(rows)
    parts = [
        rope_tables(local // (SLAB_H * WIDE), SPLITS[0]),
        rope_tables(np.zeros(rows), SPLITS[1]),
        rope_tables(local % WIDE, SPLITS[2]),
    ]
    tall = rope_tables(np.arange(heights), SPLITS[1])
    tall = [np.pad(t, ((0, 0), (SPLITS[0], SPLITS[2]))) for t in tall]
    fixed = [np.concatenate([p[i] for p in parts], 1) for i in range(2)]
    return [np.asarray(t, np.float32) for t in fixed + tall]


def prep_kernel(
    send_ref, mask_ref, slab_ref, q_ref, k_ref, v_ref, tk_ref, tv_ref, cos_ref, sin_ref, hcos_ref, hsin_ref, qg_ref, kg_ref,
    *outs, first,
):
    rows = q_ref.shape[0]
    texts = tk_ref.shape[0]
    here = lax.axis_index("seq") * lax.axis_size("tp") + lax.axis_index("tp")
    lane = lax.broadcasted_iota(jnp.int32, (rows, HEAD), 1)
    row = lax.broadcasted_iota(jnp.int32, (rows, HEAD), 0)
    in_first = lane < SPLITS[0]
    h0, h1 = SPLITS[0] // 2, SPLITS[1] // 2
    low = jnp.where(in_first, lane - h0, lax.rem(lane + SPLITS[1] - SPLITS[0], SPLITS[1]) - h1) < 0
    in_height = jnp.logical_and(lane >= SPLITS[0], lane < SPLITS[0] + SPLITS[1])
    which = lax.rem(lax.div(row, WIDE), SLAB_H)

    def table(fixed_ref, tall_ref):
        value = fixed_ref[...]
        for h in range(SLAB_H):
            mine = jnp.logical_and(in_height, which == h)
            value = jnp.where(mine, tall_ref[pl.ds(slab_ref[0] * SLAB_H + h, 1), :], value)
        return value

    cos = table(cos_ref, hcos_ref)
    sin = table(sin_ref, hsin_ref)
    marker = lax.broadcasted_iota(jnp.int32, (texts, HEAD), 0)
    marks = jnp.zeros((texts, HEAD), jnp.float32)
    for i in range(texts):
        marks = jnp.where(marker == i, mask_ref[i].astype(jnp.float32), marks)

    def norm(x, gain):
        x = x.astype(jnp.float32)
        return x * lax.rsqrt(jnp.mean(x * x, axis=-1, keepdims=True) + 0.05) * gain

    def rotate(x):
        up = jnp.where(in_first, pltpu.roll(x, HEAD - h0, 1), pltpu.roll(x, HEAD - h1, 1))
        down = jnp.where(in_first, pltpu.roll(x, h0, 1), pltpu.roll(x, h1, 1))
        return x * cos + jnp.where(low, up, down) * sin

    for r, out in enumerate(outs):
        col = pl.ds(pl.multiple_of(send_ref[here, first + r] * HEAD, HEAD), HEAD)
        q = rotate(norm(q_ref[:, col], qg_ref[...])) * np.float32(1.0 / np.sqrt(HEAD))
        out[0:rows, 0:HEAD] = q.astype(jnp.bfloat16)
        out[0:rows, HEAD : 2 * HEAD] = rotate(norm(k_ref[:, col], kg_ref[...])).astype(jnp.bfloat16)
        out[0:rows, 2 * HEAD :] = v_ref[:, col]
        tail = slice(rows, rows + texts)
        out[tail, 0:HEAD] = marks.astype(jnp.bfloat16)
        out[tail, HEAD : 2 * HEAD] = norm(tk_ref[:, col], kg_ref[...]).astype(jnp.bfloat16)
        out[tail, 2 * HEAD :] = tv_ref[:, col]


def pack_kernel(*refs):
    *ins, out = refs
    rows = out.shape[1] - PAD
    visual = ins[0].shape[0] - PAD
    for b, ref in enumerate(ins):
        out[b, 0:visual, :] = ref[0:visual, HEAD:]
        text = ref[visual:rows, HEAD:]
        marks = ref[visual:rows, 0:HEAD]
        marks = jnp.concatenate([marks, marks], axis=1)
        out[b, visual:, :] = jnp.concatenate([text.astype(jnp.float32), marks.astype(jnp.float32)], axis=0).astype(
            jnp.bfloat16
        )


def attention_kernel(*refs, tasks, chunks, rows, texts, q_tile, k_blocks, final):
    refs = list(refs)

    def take(n):
        head, refs[:] = refs[:n], refs[n:]
        return head

    kv_refs, q_refs = take(chunks), take(tasks)
    state_in = take(3) if final else None
    outs = take(tasks) if final else take(3)
    q_scr, o_scr, tk_scr, tv_scr = refs
    per = kv_refs[0].shape[0]
    tail = texts + PAD
    for r in range(tasks):
        q_scr[r * rows : (r + 1) * rows, :] = q_refs[r][0:rows, 0:HEAD]
    for c in range(chunks):
        for b in range(per):
            at = slice((c * per + b) * tail, (c * per + b + 1) * tail)
            tk_scr[at, :] = kv_refs[c][b, rows : rows + tail, 0:HEAD]
            tv_scr[at, :] = kv_refs[c][b, rows : rows + tail, HEAD:]
    n_text = chunks * per * tail
    marks = jnp.transpose(tk_scr[...].astype(jnp.float32))[0:1, :]
    marks = pltpu.roll(marks, n_text - texts, 1)
    lane = lax.broadcasted_iota(jnp.int32, (1, n_text), 1)
    bias = jnp.where((lane % tail < texts) & (marks > 0.5), 0.0, NEGATIVE)

    def score(q, k):
        return lax.dot_general(q, k, (((1,), (1,)), ((), ())), preferred_element_type=jnp.float32)

    def absorb(state, s, v):
        top, total, acc = state
        fresh = jnp.maximum(top, jnp.max(s, axis=-1, keepdims=True))
        p = jnp.exp(s - fresh)
        factor = jnp.exp(top - fresh)
        total = total * factor + jnp.sum(p, axis=-1, keepdims=True)
        acc = acc * factor + jnp.dot(p.astype(jnp.bfloat16), v, preferred_element_type=jnp.float32)
        return fresh, total, acc

    def tile(i, carry):
        at = pl.ds(pl.multiple_of(i * q_tile, q_tile), q_tile)
        q = q_scr[at, :]
        state = (
            jnp.full((q_tile, 1), NEGATIVE, jnp.float32),
            jnp.zeros((q_tile, 1), jnp.float32),
            jnp.zeros((q_tile, HEAD), jnp.float32),
        )
        spans = [(ref, slice(b, b + k_blocks)) for ref in kv_refs for b in range(0, per, k_blocks)]
        ready = score(q, tk_scr[...]) + bias
        value = tv_scr[...]
        for ref, at_b in spans:
            ahead = score(q, ref[at_b, 0:rows, 0:HEAD].reshape(k_blocks * rows, HEAD))
            state = absorb(state, ready, value)
            ready, value = ahead, ref[at_b, 0:rows, HEAD:].reshape(k_blocks * rows, HEAD)
        top, total, acc = absorb(state, ready, value)
        top = jnp.broadcast_to(top, (q_tile, HEAD))
        total = jnp.broadcast_to(total, (q_tile, HEAD))
        if final:
            top_in, total_in, acc_in = (ref[at, :] for ref in state_in)
            high = jnp.maximum(top, top_in)
            here, there = jnp.exp(top - high), jnp.exp(top_in - high)
            acc = acc * here + acc_in * there
            o_scr[at, :] = (acc / (total * here + total_in * there)).astype(jnp.bfloat16)
        else:
            outs[0][at, :] = top
            outs[1][at, :] = total
            outs[2][at, :] = acc
        return carry

    lax.fori_loop(0, tasks * rows // q_tile, tile, 0)
    if final:
        for r in range(tasks):
            outs[r][...] = o_scr[r * rows : (r + 1) * rows, :]


def attend(chunks, queries, state, rows, texts, final):
    tasks = len(queries)
    vmem = pl.BlockSpec(memory_space=pltpu.VMEM)
    many = tasks * rows
    n_text = sum(c.shape[0] for c in chunks) * (texts + PAD)
    if final:
        shapes = [jax.ShapeDtypeStruct((rows, HEAD), jnp.bfloat16)] * tasks
    else:
        shapes = [jax.ShapeDtypeStruct((many, HEAD), jnp.float32)] * 3
    extra = [] if state is None else list(state)
    return pl.pallas_call(
        functools.partial(
            attention_kernel, tasks=tasks, chunks=len(chunks), rows=rows, texts=texts, q_tile=2 * rows,
            k_blocks=tasks // 2, final=final,
        ),
        out_shape=shapes,
        in_specs=[vmem] * (len(chunks) + tasks + len(extra)),
        out_specs=[vmem] * len(shapes),
        scratch_shapes=[
            pltpu.VMEM((many, HEAD), jnp.bfloat16),
            pltpu.VMEM((many, HEAD), jnp.bfloat16),
            pltpu.VMEM((n_text, HEAD), jnp.bfloat16),
            pltpu.VMEM((n_text, HEAD), jnp.bfloat16),
        ],
        name="attention",
    )(*chunks, *queries, *extra)


def project_kernel(send_ref, valid_ref, w_ref, *refs, rounds):
    ins, (mine_ref, other_ref, joined) = refs[:rounds], refs[rounds:]
    share = mine_ref.shape[0]
    me = lax.axis_index("tp")
    here = lax.axis_index("seq") * lax.axis_size("tp") + me

    for r in range(rounds):

        @pl.when(valid_ref[here, r] == 1)
        def _():
            at = pl.ds(pl.multiple_of(send_ref[here, r] * HEAD, HEAD), HEAD)
            joined[:, at] = ins[r][...]

    first = jnp.dot(joined[...], w_ref[...], preferred_element_type=jnp.float32).astype(jnp.bfloat16)
    low, high = first[:share], first[share:]
    mine_ref[...] = jnp.where(me == 0, low, high)
    other_ref[...] = jnp.where(me == 0, high, low)


def body(
    visual_q, visual_key_input, visual_v, text_k, text_v, text_mask, slab_order, q_gain, key_norm_gain, w_out
):
    rows, width = visual_q.shape
    texts = text_k.shape[0]
    heads = width // HEAD
    n_seq, n_tp = lax.axis_size("seq"), lax.axis_size("tp")
    rounds, perms, send, valid, cross, flip = plan(n_seq, n_tp, heads)
    both = ("seq", "tp")
    full = rows + texts
    vmem = pl.BlockSpec(memory_space=pltpu.VMEM)
    smem = pl.BlockSpec(memory_space=pltpu.SMEM)
    tables = position_tables(rows, n_seq * SLAB_H)
    half = rounds // 2
    got = []
    for first in (0, half):
        blocks = pl.pallas_call(
            functools.partial(prep_kernel, first=first),
            out_shape=[jax.ShapeDtypeStruct((full, 3 * HEAD), jnp.bfloat16)] * half,
            in_specs=[smem] * 3 + [vmem] * 11,
            out_specs=[vmem] * half,
            name="prep",
        )(
            send, text_mask, slab_order, visual_q, visual_key_input, visual_v, text_k, text_v, *tables,
            q_gain.reshape(1, HEAD), key_norm_gain.reshape(1, HEAD),
        )
        for r, b in enumerate(blocks, first):
            got.append(lax.ppermute(b, both, perms[r]))
    own = pl.pallas_call(
        pack_kernel,
        out_shape=jax.ShapeDtypeStruct((rounds, full + PAD, 2 * HEAD), jnp.bfloat16),
        in_specs=[vmem] * rounds,
        out_specs=vmem,
        name="pack",
    )(*got)
    across = lax.ppermute(own, both, cross)
    peer = lax.ppermute(own, both, flip)
    state = attend([own, peer], got, None, rows, texts, False)
    peer_across = lax.ppermute(across, both, flip)
    outs = attend([across, peer_across], got, state, rows, texts, True)
    back = [None] * rounds
    for r in range(rounds):
        back[r] = lax.ppermute(outs[r], both, [(d, s) for s, d in perms[r]])
    share = rows // n_tp
    mine, other = pl.pallas_call(
        functools.partial(project_kernel, rounds=rounds),
        out_shape=[jax.ShapeDtypeStruct((share, w_out.shape[1]), jnp.bfloat16)] * 2,
        in_specs=[smem] * 2 + [vmem] * (1 + rounds),
        out_specs=[vmem] * 2,
        scratch_shapes=[pltpu.VMEM((rows, width), jnp.bfloat16)],
        name="project",
    )(send, valid, w_out, *back)
    theirs = lax.ppermute(other, "tp", [(0, 1), (1, 0)])
    return (mine.astype(jnp.float32) + theirs.astype(jnp.float32)).astype(jnp.bfloat16)


def solution(mesh):
    wide = P(("grp", "seq"), "tp")
    long = P(("grp", "seq"))
    placed = (wide, wide, wide, wide, wide, long, long, P(), P(), P("tp", None))
    return jax.shard_map(body, mesh=mesh, in_specs=placed, out_specs=P(("grp", "seq", "tp"), None), check_vma=False)
```

profile of v0, /device:TPU:37, one launch (start us, length us, event | category | flops | bytes accessed | tf_op | source)
XLA Modules:
  0.0 288.2 jit_solution(14723323034072458760)
XLA Ops:
  0.7 4.2 %prep.2 = (bf16[264,384]{1,0:T(8,128)(2,1)}, bf16[264,384]{1,0:T(8,128)(2,1)}, bf16[264,384]{1,0:T(8,128)(2,1)}, bf16[264,384]{1,0:T(8,128)(2,1)}) custom-call(s32[64,8]{1,0:T(8,128)} %constant.12.clone.send_ref, s32[8]{0:T(128)} %mask_ref.3, s32[1]{0:T(128)S(6)} %copy.17.slab_ref, bf16[256,768]{1,0:T(8,128)(2,1)} %q_ref.3, bf16[256,768]{1,0:T(8,128)(2,1)} %k_ref.3, ...), custom_call_target="tpu_custom_call" | custom-call | tf_op jit(solution)/shard_map/prep/pallas_call | solution.py:369
  4.9 1.3 collective-permute-start
  6.2 30.8 %collective-permute-start.1 = (bf16[264,384]{1,0:T(8,128)(2,1)}, bf16[264,384]{1,0:T(8,128)(2,1)S(1)}, u32[]{:S(2)}, u32[]{:S(2)}) collective-permute-start(bf16[264,384]{1,0:T(8,128)(2,1)} %get-tuple-element.27), channel_id=1, source_target_pairs={{0,0},{1,61},{2,2},{3,5},{4,3},{5,4},{7,6},{8,11},{9,7},{10,10},{1... | collective-permute-start | bytes 608264 | tf_op jit(solution)/shard_map/ppermute | solution.py:380
  37.0 10.6 %collective-permute-start.2 = (bf16[264,384]{1,0:T(8,128)(2,1)}, bf16[264,384]{1,0:T(8,128)(2,1)S(1)}, u32[]{:S(2)}, u32[]{:S(2)}) collective-permute-start(bf16[264,384]{1,0:T(8,128)(2,1)} %get-tuple-element.28), channel_id=1, source_target_pairs={{0,20},{1,27},{3,26},{4,44},{6,45},{7,50},{8,32},{9,51},{10,33},{1... | collective-permute-start | bytes 608264 | tf_op jit(solution)/shard_map/ppermute | solution.py:380
  47.6 2.0 collective-permute-start.3
  49.6 4.3 %prep.3 = (bf16[264,384]{1,0:T(8,128)(2,1)}, bf16[264,384]{1,0:T(8,128)(2,1)}, bf16[264,384]{1,0:T(8,128)(2,1)}, bf16[264,384]{1,0:T(8,128)(2,1)}) custom-call(s32[64,8]{1,0:T(8,128)} %constant.12.clone.send_ref, s32[8]{0:T(128)} %mask_ref.3, s32[1]{0:T(128)S(6)} %copy.17.slab_ref, bf16[256,768]{1,0:T(8,128)(2,1)} %q_ref.3, bf16[256,768]{1,0:T(8,128)(2,1)} %k_ref.3, ...), custom_call_target="tpu_custom_call" | custom-call | tf_op jit(solution)/shard_map/prep/pallas_call | solution.py:369
  53.8 1.9 collective-permute-start.4
  55.8 0.0 copy-start
  55.8 67.5 %collective-permute-start.5 = (bf16[264,384]{1,0:T(8,128)(2,1)}, bf16[264,384]{1,0:T(8,128)(2,1)S(1)}, u32[]{:S(2)}, u32[]{:S(2)}) collective-permute-start(bf16[264,384]{1,0:T(8,128)(2,1)} %get-tuple-element.31), channel_id=1, source_target_pairs={{0,11},{1,50},{2,54},{5,60},{6,10},{7,61},{8,20},{9,16},{10,2},{11... | collective-permute-start | bytes 608264 | tf_op jit(solution)/shard_map/ppermute | solution.py:380
  123.3 0.0 collective-permute-done.1.refs_1_.refs_3_
  123.4 2.0 collective-permute-start.6
  125.3 0.0 collective-permute-done.2.refs_2_.refs_4_
  125.3 1.3 collective-permute-start.7
  126.7 0.0 collective-permute-done.3.refs_3_.refs_5_
  126.7 0.0 collective-permute-done.4.refs_4_.refs_6_
  126.7 15.0 %collective-permute-done.5.refs_5_.refs_7_ = bf16[264,384]{1,0:T(8,128)(2,1)S(1)} collective-permute-done((bf16[264,384]{1,0:T(8,128)(2,1)}, bf16[264,384]{1,0:T(8,128)(2,1)S(1)}, u32[]{:S(2)}, u32[]{:S(2)}) %collective-permute-start.5) | collective-permute-done | bytes 202784 | tf_op jit(solution)/shard_map/ppermute | solution.py:380
  141.7 1.7 collective-permute-done.6.refs_6_.refs_8_
  143.4 3.5 %collective-permute-done.7.refs_7_.refs_9_ = bf16[264,384]{1,0:T(8,128)(2,1)S(1)} collective-permute-done((bf16[264,384]{1,0:T(8,128)(2,1)}, bf16[264,384]{1,0:T(8,128)(2,1)S(1)}, u32[]{:S(2)}, u32[]{:S(2)}) %collective-permute-start.7) | collective-permute-done | bytes 202784 | tf_op jit(solution)/shard_map/ppermute | solution.py:380
  147.0 0.7 copy-done.7
  147.7 2.6 pack.1.refs_0_
  150.2 1.9 collective-permute-start.8
  152.2 6.9 %collective-permute-start.10 = (bf16[8,272,256]{2,1,0:T(8,128)(2,1)}, bf16[8,272,256]{2,1,0:T(8,128)(2,1)S(1)}, u32[]{:S(2)}, u32[]{:S(2)}) collective-permute-start(bf16[8,272,256]{2,1,0:T(8,128)(2,1)} %pack.1.refs_0_), channel_id=1, source_target_pairs={{0,1},{2,3},{1,0},{3,2},{4,5},{6,7},{5,4},{7,6},{10,11},{12,13},{1... | collective-permute-start | bytes 3342344 | tf_op jit(solution)/shard_map/ppermute | solution.py:389
  159.1 16.5 %collective-permute-done.8.refs_0_ = bf16[8,272,256]{2,1,0:T(8,128)(2,1)S(1)} collective-permute-done((bf16[8,272,256]{2,1,0:T(8,128)(2,1)}, bf16[8,272,256]{2,1,0:T(8,128)(2,1)S(1)}, u32[]{:S(2)}, u32[]{:S(2)}) %collective-permute-start.8) | collective-permute-done | bytes 1114144 | tf_op jit(solution)/shard_map/ppermute | solution.py:388
  175.5 5.9 %collective-permute-start.9 = (bf16[8,272,256]{2,1,0:T(8,128)(2,1)S(1)}, bf16[8,272,256]{2,1,0:T(8,128)(2,1)S(1)}, u32[]{:S(2)}, u32[]{:S(2)}) collective-permute-start(bf16[8,272,256]{2,1,0:T(8,128)(2,1)S(1)} %collective-permute-done.8.refs_0_), channel_id=1, source_target_pairs={{0,1},{2,3},{1,0},{3,2},{4,5},{6,7},{5,4},{7,6},{10,11},{12,13},{1... | collective-permute-start | bytes 3342344 | tf_op jit(solution)/shard_map/ppermute | solution.py:391
  181.5 1.0 copy-done.10
  182.5 16.0 %attention.2 = (f32[2048,128]{1,0:T(8,128)}, f32[2048,128]{1,0:T(8,128)}, f32[2048,128]{1,0:T(8,128)}) custom-call(bf16[8,272,256]{2,1,0:T(8,128)(2,1)} %pack.1.refs_0_, bf16[8,272,256]{2,1,0:T(8,128)(2,1)} %copy-done.10, bf16[264,384]{1,0:T(8,128)(2,1)} %copy-done, bf16[264,384]{1,0:T(8,128)(2,1)} %copy-done.1, bf16[264,384]{1,0:T(8,128)(2,1)} %copy-done.2, ...), custom_call_target="tpu_custom_call" | custom-call | tf_op jit(solution)/shard_map/attention/pallas_call | solution.py:316
  198.5 0.0 collective-permute-done.9.refs_1_
  198.5 1.0 copy-done.9
  199.5 16.8 %attention.3 = (bf16[256,128]{1,0:T(8,128)(2,1)}, bf16[256,128]{1,0:T(8,128)(2,1)}, bf16[256,128]{1,0:T(8,128)(2,1)}, bf16[256,128]{1,0:T(8,128)(2,1)}, bf16[256...) custom-call(bf16[8,272,256]{2,1,0:T(8,128)(2,1)} %copy-done.8, ...), custom_call_target="tpu_custom_call" | custom-call | tf_op jit(solution)/shard_map/attention/pallas_call | solution.py:316
  216.4 11.7 %collective-permute-start.11 = (bf16[256,128]{1,0:T(8,128)(2,1)}, bf16[256,128]{1,0:T(8,128)(2,1)S(1)}, u32[]{:S(2)}, u32[]{:S(2)}) collective-permute-start(bf16[256,128]{1,0:T(8,128)(2,1)} %get-tuple-element.37), channel_id=1, source_target_pairs={{35,0},{32,2},{38,3},{33,4},{39,5},{37,7},{44,8},{36,9},{45,10},{4... | collective-permute-start | bytes 196616 | tf_op jit(solution)/shard_map/ppermute | solution.py:395
  228.0 2.0 collective-permute-start.12
  230.0 15.0 %collective-permute-start.13 = (bf16[256,128]{1,0:T(8,128)(2,1)}, bf16[256,128]{1,0:T(8,128)(2,1)S(1)}, u32[]{:S(2)}, u32[]{:S(2)}) collective-permute-start(bf16[256,128]{1,0:T(8,128)(2,1)} %get-tuple-element.39), channel_id=1, source_target_pairs={{20,0},{27,1},{26,3},{44,4},{45,6},{50,7},{32,8},{51,9},{33,10},{3... | collective-permute-start | bytes 196616 | tf_op jit(solution)/shard_map/ppermute | solution.py:395
  245.0 2.0 collective-permute-start.14
  246.9 4.1 %collective-permute-start.15 = (bf16[256,128]{1,0:T(8,128)(2,1)}, bf16[256,128]{1,0:T(8,128)(2,1)S(1)}, u32[]{:S(2)}, u32[]{:S(2)}) collective-permute-start(bf16[256,128]{1,0:T(8,128)(2,1)} %get-tuple-element.41), channel_id=1, source_target_pairs={{44,0},{39,1},{45,2},{27,5},{33,6},{26,7},{54,10},{50,11},{55,12},... | collective-permute-start | bytes 196616 | tf_op jit(solution)/shard_map/ppermute | solution.py:395
  251.0 0.0 collective-permute-done.11.refs_0_
  251.1 2.0 collective-permute-start.16
  253.0 0.0 collective-permute-done.12.refs_1_
  253.0 7.1 %collective-permute-start.17 = (bf16[256,128]{1,0:T(8,128)(2,1)}, bf16[256,128]{1,0:T(8,128)(2,1)S(1)}, u32[]{:S(2)}, u32[]{:S(2)}) collective-permute-start(bf16[256,128]{1,0:T(8,128)(2,1)} %get-tuple-element.43), channel_id=1, source_target_pairs={{16,1},{21,2},{50,3},{20,4},{51,5},{54,6},{55,8},{60,9},{26,11},{3... | collective-permute-start | bytes 196616 | tf_op jit(solution)/shard_map/ppermute | solution.py:395
  260.2 0.0 collective-permute-done.13.refs_2_
  260.2 15.8 %collective-permute-start.18 = (bf16[256,128]{1,0:T(8,128)(2,1)}, bf16[256,128]{1,0:T(8,128)(2,1)S(1)}, u32[]{:S(2)}, u32[]{:S(2)}) collective-permute-start(bf16[256,128]{1,0:T(8,128)(2,1)} %get-tuple-element.44), channel_id=1, source_target_pairs={{54,0},{17,3},{55,4},{16,5},{21,6},{26,9},{20,10},{61,11},{3,12},{... | collective-permute-start | bytes 196616 | tf_op jit(solution)/shard_map/ppermute | solution.py:395
  276.0 0.0 collective-permute-done.14.refs_3_
  276.0 0.0 collective-permute-done.15.refs_4_
  276.1 0.0 collective-permute-done.17.refs_6_
  276.1 1.5 collective-permute-done.18.refs_7_
  277.7 0.6 copy-done.18
  278.3 5.2 %project.1 = (bf16[128,3072]{1,0:T(8,128)(2,1)}, bf16[128,3072]{1,0:T(8,128)(2,1)}) custom-call(s32[64,8]{1,0:T(8,128)} %constant.12.clone.send_ref, s32[64,8]{1,0:T(8,128)} %constant.17.clone.valid_ref, bf16[768,3072]{1,0:T(8,128)(2,1)} %w_ref.1, bf16[256,128]{1,0:T(8,128)(2,1)} %copy-done.11, bf16[256,128]{1,0:T(8,128)(2,1)} %copy-done.12, ...), custom_call_target="tpu_custom_call" | custom-call | tf_op jit(solution)/shard_map/project/pallas_call | solution.py:397
  283.5 2.5 collective-permute-done.19
  286.0 2.2 add_convert_fusion
  (37 shorter events, 0.1 us)
Async XLA Ops:
  4.9 50.9 %collective-permute-start = (bf16[264,384]{1,0:T(8,128)(2,1)}, bf16[264,384]{1,0:T(8,128)(2,1)S(1)}, u32[]{:S(2)}, u32[]{:S(2)}) collective-permute-start(bf16[264,384]{1,0:T(8,128)(2,1)} %get-tuple-element.26), channel_id=1, source_target_pairs={{0,35},{2,32},{3,38},{4,33},{5,39},{7,37},{8,44},{9,36},{10,45},{1... | collective-permute-start | bytes 608264 | tf_op jit(solution)/shard_map/ppermute | solution.py:380
  6.2 117.2 %collective-permute-start.1 = (bf16[264,384]{1,0:T(8,128)(2,1)}, bf16[264,384]{1,0:T(8,128)(2,1)S(1)}, u32[]{:S(2)}, u32[]{:S(2)}) collective-permute-start(bf16[264,384]{1,0:T(8,128)(2,1)} %get-tuple-element.27), channel_id=1, source_target_pairs={{0,0},{1,61},{2,2},{3,5},{4,3},{5,4},{7,6},{8,11},{9,7},{10,10},{1... | collective-permute-start | bytes 608264 | tf_op jit(solution)/shard_map/ppermute | solution.py:380
  37.0 88.3 %collective-permute-start.2 = (bf16[264,384]{1,0:T(8,128)(2,1)}, bf16[264,384]{1,0:T(8,128)(2,1)S(1)}, u32[]{:S(2)}, u32[]{:S(2)}) collective-permute-start(bf16[264,384]{1,0:T(8,128)(2,1)} %get-tuple-element.28), channel_id=1, source_target_pairs={{0,20},{1,27},{3,26},{4,44},{6,45},{7,50},{8,32},{9,51},{10,33},{1... | collective-permute-start | bytes 608264 | tf_op jit(solution)/shard_map/ppermute | solution.py:380
  47.6 79.1 %collective-permute-start.3 = (bf16[264,384]{1,0:T(8,128)(2,1)}, bf16[264,384]{1,0:T(8,128)(2,1)S(1)}, u32[]{:S(2)}, u32[]{:S(2)}) collective-permute-start(bf16[264,384]{1,0:T(8,128)(2,1)} %get-tuple-element.29), channel_id=1, source_target_pairs={{1,4},{2,11},{3,61},{4,10},{6,2},{7,17},{8,3},{11,6},{13,16},{14,2... | collective-permute-start | bytes 608264 | tf_op jit(solution)/shard_map/ppermute | solution.py:380
  53.8 72.9 %collective-permute-start.4 = (bf16[264,384]{1,0:T(8,128)(2,1)}, bf16[264,384]{1,0:T(8,128)(2,1)S(1)}, u32[]{:S(2)}, u32[]{:S(2)}) collective-permute-start(bf16[264,384]{1,0:T(8,128)(2,1)} %get-tuple-element.30), channel_id=1, source_target_pairs={{0,44},{1,39},{2,45},{5,27},{6,33},{7,26},{10,54},{11,50},{12,55},... | collective-permute-start | bytes 608264 | tf_op jit(solution)/shard_map/ppermute | solution.py:380
  55.8 91.1 %copy-start = (bf16[264,384]{1,0:T(8,128)(2,1)}, bf16[264,384]{1,0:T(8,128)(2,1)S(1)}, u32[]{:S(2)}) copy-start(bf16[264,384]{1,0:T(8,128)(2,1)S(1)} %collective-permute-done.refs_0_.refs_2_) | copy-start | bytes 608260
  55.8 85.9 %collective-permute-start.5 = (bf16[264,384]{1,0:T(8,128)(2,1)}, bf16[264,384]{1,0:T(8,128)(2,1)S(1)}, u32[]{:S(2)}, u32[]{:S(2)}) collective-permute-start(bf16[264,384]{1,0:T(8,128)(2,1)} %get-tuple-element.31), channel_id=1, source_target_pairs={{0,11},{1,50},{2,54},{5,60},{6,10},{7,61},{8,20},{9,16},{10,2},{11... | collective-permute-start | bytes 608264 | tf_op jit(solution)/shard_map/ppermute | solution.py:380
  123.4 23.6 %copy-start.1 = (bf16[264,384]{1,0:T(8,128)(2,1)}, bf16[264,384]{1,0:T(8,128)(2,1)S(1)}, u32[]{:S(2)}) copy-start(bf16[264,384]{1,0:T(8,128)(2,1)S(1)} %collective-permute-done.1.refs_1_.refs_3_) | copy-start | bytes 608260
  123.4 20.0 %collective-permute-start.6 = (bf16[264,384]{1,0:T(8,128)(2,1)}, bf16[264,384]{1,0:T(8,128)(2,1)S(1)}, u32[]{:S(2)}, u32[]{:S(2)}) collective-permute-start(bf16[264,384]{1,0:T(8,128)(2,1)} %get-tuple-element.32), channel_id=1, source_target_pairs={{1,16},{2,21},{3,50},{4,20},{5,51},{6,54},{8,55},{9,60},{11,26},{1... | collective-permute-start | bytes 608264 | tf_op jit(solution)/shard_map/ppermute | solution.py:380
  125.3 21.6 %copy-start.2 = (bf16[264,384]{1,0:T(8,128)(2,1)}, bf16[264,384]{1,0:T(8,128)(2,1)S(1)}, u32[]{:S(2)}) copy-start(bf16[264,384]{1,0:T(8,128)(2,1)S(1)} %collective-permute-done.2.refs_2_.refs_4_) | copy-start | bytes 608260
  125.3 21.6 %collective-permute-start.7 = (bf16[264,384]{1,0:T(8,128)(2,1)}, bf16[264,384]{1,0:T(8,128)(2,1)S(1)}, u32[]{:S(2)}, u32[]{:S(2)}) collective-permute-start(bf16[264,384]{1,0:T(8,128)(2,1)} %get-tuple-element.33), channel_id=1, source_target_pairs={{0,54},{3,17},{4,55},{5,16},{6,21},{9,26},{10,20},{11,61},{12,3},{... | collective-permute-start | bytes 608264 | tf_op jit(solution)/shard_map/ppermute | solution.py:380
  126.7 20.3 %copy-start.3 = (bf16[264,384]{1,0:T(8,128)(2,1)}, bf16[264,384]{1,0:T(8,128)(2,1)S(1)}, u32[]{:S(2)}) copy-start(bf16[264,384]{1,0:T(8,128)(2,1)S(1)} %collective-permute-done.3.refs_3_.refs_5_) | copy-start | bytes 608260
  126.7 20.3 %copy-start.4 = (bf16[264,384]{1,0:T(8,128)(2,1)}, bf16[264,384]{1,0:T(8,128)(2,1)S(1)}, u32[]{:S(2)}) copy-start(bf16[264,384]{1,0:T(8,128)(2,1)S(1)} %collective-permute-done.4.refs_4_.refs_6_) | copy-start | bytes 608260
  141.7 5.3 %copy-start.5 = (bf16[264,384]{1,0:T(8,128)(2,1)}, bf16[264,384]{1,0:T(8,128)(2,1)S(1)}, u32[]{:S(2)}) copy-start(bf16[264,384]{1,0:T(8,128)(2,1)S(1)} %collective-permute-done.5.refs_5_.refs_7_) | copy-start | bytes 608260
  143.4 3.6 %copy-start.6 = (bf16[264,384]{1,0:T(8,128)(2,1)}, bf16[264,384]{1,0:T(8,128)(2,1)S(1)}, u32[]{:S(2)}) copy-start(bf16[264,384]{1,0:T(8,128)(2,1)S(1)} %collective-permute-done.6.refs_6_.refs_8_) | copy-start | bytes 608260
  147.0 0.7 copy-start.7
  150.2 25.3 %collective-permute-start.8 = (bf16[8,272,256]{2,1,0:T(8,128)(2,1)}, bf16[8,272,256]{2,1,0:T(8,128)(2,1)S(1)}, u32[]{:S(2)}, u32[]{:S(2)}) collective-permute-start(bf16[8,272,256]{2,1,0:T(8,128)(2,1)} %pack.1.refs_0_), channel_id=1, source_target_pairs={{0,2},{2,0},{1,3},{3,1},{4,6},{6,4},{5,7},{7,5},{10,12},{12,10},{1... | collective-permute-start | bytes 3342344 | tf_op jit(solution)/shard_map/ppermute | solution.py:388
  152.2 29.3 %collective-permute-start.10 = (bf16[8,272,256]{2,1,0:T(8,128)(2,1)}, bf16[8,272,256]{2,1,0:T(8,128)(2,1)S(1)}, u32[]{:S(2)}, u32[]{:S(2)}) collective-permute-start(bf16[8,272,256]{2,1,0:T(8,128)(2,1)} %pack.1.refs_0_), channel_id=1, source_target_pairs={{0,1},{2,3},{1,0},{3,2},{4,5},{6,7},{5,4},{7,6},{10,11},{12,13},{1... | collective-permute-start | bytes 3342344 | tf_op jit(solution)/shard_map/ppermute | solution.py:389
  175.5 23.0 %copy-start.8 = (bf16[8,272,256]{2,1,0:T(8,128)(2,1)}, bf16[8,272,256]{2,1,0:T(8,128)(2,1)S(1)}, u32[]{:S(2)}) copy-start(bf16[8,272,256]{2,1,0:T(8,128)(2,1)S(1)} %collective-permute-done.8.refs_0_) | copy-start | bytes 3342340
  175.5 23.0 %collective-permute-start.9 = (bf16[8,272,256]{2,1,0:T(8,128)(2,1)S(1)}, bf16[8,272,256]{2,1,0:T(8,128)(2,1)S(1)}, u32[]{:S(2)}, u32[]{:S(2)}) collective-permute-start(bf16[8,272,256]{2,1,0:T(8,128)(2,1)S(1)} %collective-permute-done.8.refs_0_), channel_id=1, source_target_pairs={{0,1},{2,3},{1,0},{3,2},{4,5},{6,7},{5,4},{7,6},{10,11},{12,13},{1... | collective-permute-start | bytes 3342344 | tf_op jit(solution)/shard_map/ppermute | solution.py:391
  181.5 1.0 copy-start.10
  198.5 1.0 copy-start.9
  216.4 34.7 %collective-permute-start.11 = (bf16[256,128]{1,0:T(8,128)(2,1)}, bf16[256,128]{1,0:T(8,128)(2,1)S(1)}, u32[]{:S(2)}, u32[]{:S(2)}) collective-permute-start(bf16[256,128]{1,0:T(8,128)(2,1)} %get-tuple-element.37), channel_id=1, source_target_pairs={{35,0},{32,2},{38,3},{33,4},{39,5},{37,7},{44,8},{36,9},{45,10},{4... | collective-permute-start | bytes 196616 | tf_op jit(solution)/shard_map/ppermute | solution.py:395
  228.0 25.0 %collective-permute-start.12 = (bf16[256,128]{1,0:T(8,128)(2,1)}, bf16[256,128]{1,0:T(8,128)(2,1)S(1)}, u32[]{:S(2)}, u32[]{:S(2)}) collective-permute-start(bf16[256,128]{1,0:T(8,128)(2,1)} %get-tuple-element.38), channel_id=1, source_target_pairs={{0,0},{61,1},{2,2},{5,3},{3,4},{4,5},{6,7},{11,8},{7,9},{10,10},{1... | collective-permute-start | bytes 196616 | tf_op jit(solution)/shard_map/ppermute | solution.py:395
  230.0 30.1 %collective-permute-start.13 = (bf16[256,128]{1,0:T(8,128)(2,1)}, bf16[256,128]{1,0:T(8,128)(2,1)S(1)}, u32[]{:S(2)}, u32[]{:S(2)}) collective-permute-start(bf16[256,128]{1,0:T(8,128)(2,1)} %get-tuple-element.39), channel_id=1, source_target_pairs={{20,0},{27,1},{26,3},{44,4},{45,6},{50,7},{32,8},{51,9},{33,10},{3... | collective-permute-start | bytes 196616 | tf_op jit(solution)/shard_map/ppermute | solution.py:395
  245.0 31.0 %collective-permute-start.14 = (bf16[256,128]{1,0:T(8,128)(2,1)}, bf16[256,128]{1,0:T(8,128)(2,1)S(1)}, u32[]{:S(2)}, u32[]{:S(2)}) collective-permute-start(bf16[256,128]{1,0:T(8,128)(2,1)} %get-tuple-element.40), channel_id=1, source_target_pairs={{4,1},{11,2},{61,3},{10,4},{2,6},{17,7},{3,8},{6,11},{16,13},{21,1... | collective-permute-start | bytes 196616 | tf_op jit(solution)/shard_map/ppermute | solution.py:395
  246.9 29.1 %collective-permute-start.15 = (bf16[256,128]{1,0:T(8,128)(2,1)}, bf16[256,128]{1,0:T(8,128)(2,1)S(1)}, u32[]{:S(2)}, u32[]{:S(2)}) collective-permute-start(bf16[256,128]{1,0:T(8,128)(2,1)} %get-tuple-element.41), channel_id=1, source_target_pairs={{44,0},{39,1},{45,2},{27,5},{33,6},{26,7},{54,10},{50,11},{55,12},... | collective-permute-start | bytes 196616 | tf_op jit(solution)/shard_map/ppermute | solution.py:395
  251.1 26.6 %copy-start.11 = (bf16[256,128]{1,0:T(8,128)(2,1)}, bf16[256,128]{1,0:T(8,128)(2,1)S(1)}, u32[]{:S(2)}) copy-start(bf16[256,128]{1,0:T(8,128)(2,1)S(1)} %collective-permute-done.11.refs_0_) | copy-start | bytes 196612
  251.1 25.0 %collective-permute-start.16 = (bf16[256,128]{1,0:T(8,128)(2,1)}, bf16[256,128]{1,0:T(8,128)(2,1)S(1)}, u32[]{:S(2)}, u32[]{:S(2)}) collective-permute-start(bf16[256,128]{1,0:T(8,128)(2,1)} %get-tuple-element.42), channel_id=1, source_target_pairs={{11,0},{50,1},{54,2},{60,5},{10,6},{61,7},{20,8},{16,9},{2,10},{17... | collective-permute-start | bytes 196616 | tf_op jit(solution)/shard_map/ppermute | solution.py:395
  253.0 24.6 %copy-start.12 = (bf16[256,128]{1,0:T(8,128)(2,1)}, bf16[256,128]{1,0:T(8,128)(2,1)S(1)}, u32[]{:S(2)}) copy-start(bf16[256,128]{1,0:T(8,128)(2,1)S(1)} %collective-permute-done.12.refs_1_) | copy-start | bytes 196612
  253.0 23.0 %collective-permute-start.17 = (bf16[256,128]{1,0:T(8,128)(2,1)}, bf16[256,128]{1,0:T(8,128)(2,1)S(1)}, u32[]{:S(2)}, u32[]{:S(2)}) collective-permute-start(bf16[256,128]{1,0:T(8,128)(2,1)} %get-tuple-element.43), channel_id=1, source_target_pairs={{16,1},{21,2},{50,3},{20,4},{51,5},{54,6},{55,8},{60,9},{26,11},{3... | collective-permute-start | bytes 196616 | tf_op jit(solution)/shard_map/ppermute | solution.py:395
  260.2 17.5 %copy-start.13 = (bf16[256,128]{1,0:T(8,128)(2,1)}, bf16[256,128]{1,0:T(8,128)(2,1)S(1)}, u32[]{:S(2)}) copy-start(bf16[256,128]{1,0:T(8,128)(2,1)S(1)} %collective-permute-done.13.refs_2_) | copy-start | bytes 196612
  260.2 17.4 %collective-permute-start.18 = (bf16[256,128]{1,0:T(8,128)(2,1)}, bf16[256,128]{1,0:T(8,128)(2,1)S(1)}, u32[]{:S(2)}, u32[]{:S(2)}) collective-permute-start(bf16[256,128]{1,0:T(8,128)(2,1)} %get-tuple-element.44), channel_id=1, source_target_pairs={{54,0},{17,3},{55,4},{16,5},{21,6},{26,9},{20,10},{61,11},{3,12},{... | collective-permute-start | bytes 196616 | tf_op jit(solution)/shard_map/ppermute | solution.py:395
  276.0 1.6 copy-start.14
  276.0 1.6 copy-start.15
  276.0 1.6 copy-start.16
  276.1 1.6 copy-start.17
  277.7 0.6 copy-start.18
  283.5 2.5 collective-permute-start.19
where the time goes:
time: 290 us; the launch traced here: 288 us
  starting transfers between devices  192 us (66%)
  Pallas kernels  49.2 us (17%)
  waiting for transfers between devices  40.8 us (14%)
  local copies, waits for them, and re-layouts  3.35 us (1%)
    ppermute x8, starting transfers between devices, body(): got.append(lax.ppermute(b, both, perms[r]))  117 us
    ppermute x8, starting transfers between devices, body(): back[r] = lax.ppermute(outs[r], both, [(d, s) for s, d in perms[r]])  59.5 us
    pallas_call x2, Pallas kernels, attend(): pl.pallas_call(functools.partial(attention_kernel, tasks=tasks, chunks=le...  32.9 us
    ppermute x8, waiting for transfers between devices, body(): got.append(lax.ppermute(b, both, perms[r]))  20.2 us
    ppermute x1, waiting for transfers between devices, body(): across = lax.ppermute(own, both, cross)  16.5 us
    pallas_call x2, Pallas kernels, body(): pl.pallas_call(functools.partial(prep_kernel, first=first), out_shape=[ja...  8.51 us
    ppermute x1, starting transfers between devices, body(): peer = lax.ppermute(own, both, flip)  6.88 us
    ppermute x1, starting transfers between devices, body(): peer_across = lax.ppermute(across, both, flip)  5.9 us
  transfers between devices with their start and end apart: 20, of which 6 were waited for; matrix products, arithmetic and copies ran while one was open for 0% of the time, Pallas kernels for 7%

commit v1 on v0

--- a/solution.py
+++ b/solution.py
@@ -46,7 +46,7 @@
     return at_src
 
 
-def sort_rounds(at_src, at_dst, colors, n_tp, cost):
+def sort_rounds(at_src, at_dst, colors, cost):
     for _ in range(20):
         moved = False
         for a in range(colors):
@@ -75,20 +75,6 @@
                         for s, d, c in edges:
                             at_src[s][a + b - c] = d
                             at_dst[d][a + b - c] = s
-        for chip in sorted({d // n_tp for d in at_dst}):
-            slots = [(d, r) for d in sorted(at_dst) if d // n_tp == chip for r in range(colors)]
-            for i in range(len(slots)):
-                for j in range(i):
-                    (d1, r1), (d2, r2) = slots[i], slots[j]
-                    s1, s2 = at_dst[d1][r1], at_dst[d2][r2]
-                    if r1 == r2 or s1 == s2 or r2 in at_src[s1] or r1 in at_src[s2]:
-                        continue
-                    before = cost(s1, d1, r1) + cost(s2, d2, r2)
-                    if cost(s1, d2, r2) + cost(s2, d1, r1) < before - 1e-6:
-                        moved = True
-                        del at_src[s1][r1], at_src[s2][r2]
-                        at_src[s1][r2], at_src[s2][r1] = d2, d1
-                        at_dst[d1][r1], at_dst[d2][r2] = s2, s1
         if not moved:
             break
 
@@ -97,43 +83,68 @@
     total = heads * n_tp
     chips = 2
     rounds = n_seq // (chips * n_tp)
-    owner = {}
-    for arc in range(total):
-        start = arc * n_seq // total
-        tp, local = arc % n_tp, arc // n_tp
+    backs = rounds // 2
+    owner, local_of, back_edges, task_of, swap = {}, {}, [], {}, []
+    for pair in range(total // 2):
+        tp = pair % n_tp
+        starts = [arc * n_seq // total for arc in (2 * pair, 2 * pair + 1)]
+        middle = (starts[0] + starts[1] + 2) // 2
         for z in range(n_seq):
-            rel = (z - start - 1) % n_seq
-            near, chip = (rel, start + 1) if rel < n_seq // 2 else (n_seq - 1 - rel, start)
-            owner[(z * n_tp + tp, local)] = chip % n_seq * n_tp + near % n_tp
-    at_src = color_edges(sorted((src, dst) for (src, _), dst in owner.items()), rounds)
-    at_dst = {}
-    for src, table in at_src.items():
-        for r, dst in table.items():
-            at_dst.setdefault(dst, {})[r] = src
+            rel = (z - middle) % n_seq
+            near, right = (rel, 1) if rel < n_seq // 2 else (n_seq - 1 - rel, 0)
+            src = z * n_tp + tp
+            devices = [(start + right) % n_seq * n_tp + near % n_tp for start in starts]
+            for side in range(2):
+                local = pair // n_tp * 2 + side
+                owner[(src, local)] = devices[side]
+                local_of[(src, devices[side])] = local
+            keep = right ^ (near < n_seq // 4)
+            back_edges.append((src, devices[keep]))
+            task_of[(src, devices[keep])] = devices[1 - keep]
+            if near < n_tp:
+                swap += [tuple(devices), tuple(reversed(devices))]
 
     def hops(src, dst):
         apart = abs(src // n_tp - dst // n_tp)
         return min(apart, n_seq - apart)
 
-    per_round = n_seq / 2 / rounds
-    for power in (1, 2, 3, 4):
-        sort_rounds(
-            at_src, at_dst, rounds, n_tp, lambda s, d, c: abs(hops(s, d) - per_round * (c + 0.25)) ** power
-        )
+    def sorted_rounds(edges, colors):
+        at_src = color_edges(sorted(edges), colors)
+        at_dst = {}
+        for src, table in at_src.items():
+            for r, dst in table.items():
+                at_dst.setdefault(dst, {})[r] = src
+        per_round = n_seq / 2 / colors
+        for power in (1, 2, 3, 4):
+            sort_rounds(
+                at_src, at_dst, colors, lambda s, d, c: abs(hops(s, d) - per_round * (c + 0.25)) ** power
+            )
+        return at_src
+
     order = [r for pair in zip(reversed(range(rounds // 2, rounds)), range(rounds // 2)) for r in pair]
-    local_of = {}
-    for (src, local), dst in owner.items():
-        local_of.setdefault((src, dst // n_tp), []).append(local)
     perms = [[] for _ in range(rounds)]
     send = np.zeros((n_seq * n_tp, rounds), np.int32)
-    valid = np.zeros((n_seq * n_tp, rounds), np.int32)
-    for src in sorted(at_src):
-        for r, dst in sorted(at_src[src].items()):
-            (local,) = local_of[(src, dst // n_tp)]
+    slot_of = {}
+    for src, table in sorted(sorted_rounds([(s, d) for (s, _), d in owner.items()], rounds).items()):
+        for r, dst in sorted(table.items()):
             slot = order.index(r)
             perms[slot].append((src, dst))
-            send[src, slot] = local
-            valid[src, slot] = 1
+            send[src, slot] = local_of[(src, dst)]
+            slot_of[(src, dst)] = slot
+    perms_back = [[] for _ in range(backs)]
+    place = np.tile(np.arange(rounds, dtype=np.int32), (n_seq * n_tp, 1))
+    heads_back = np.zeros((n_seq * n_tp, 2 * backs), np.int32)
+    valid = np.zeros((n_seq * n_tp, backs), np.int32)
+    for src, table in sorted(sorted_rounds(back_edges, backs).items()):
+        for r, dst in sorted(table.items()):
+            j = backs - 1 - r
+            other = task_of[(src, dst)]
+            perms_back[j].append((dst, src))
+            place[dst, slot_of[(src, dst)]] = backs + j
+            place[other, slot_of[(src, other)]] = j
+            heads_back[src, 2 * j] = local_of[(src, dst)]
+            heads_back[src, 2 * j + 1] = local_of[(src, other)]
+            valid[src, j] = 1
     cross, flip = [], []
     for arc in range(total):
         start = arc * n_seq // total
@@ -141,7 +152,7 @@
         for t in range(n_tp):
             cross += [(start * n_tp + t, after * n_tp + t), (after * n_tp + t, start * n_tp + t)]
             flip += [(chip * n_tp + t, chip * n_tp + (t + 1) % n_tp) for chip in (start, after)]
-    return rounds, perms, send, valid, cross, flip
+    return perms, send, cross, flip, place, sorted(set(swap)), perms_back, heads_back, valid
 
 
 def rope_tables(positions, size):
@@ -229,27 +240,18 @@
         )
 
 
-def attention_kernel(*refs, tasks, chunks, rows, texts, q_tile, k_blocks, final):
-    refs = list(refs)
-
-    def take(n):
-        head, refs[:] = refs[:n], refs[n:]
-        return head
-
-    kv_refs, q_refs = take(chunks), take(tasks)
-    state_in = take(3) if final else None
-    outs = take(tasks) if final else take(3)
-    q_scr, o_scr, tk_scr, tv_scr = refs
+def attend(q_ref, kv_refs, tk_scr, v_scr, rows, texts, q_tile, k_blocks, finish):
     per = kv_refs[0].shape[0]
     tail = texts + PAD
-    for r in range(tasks):
-        q_scr[r * rows : (r + 1) * rows, :] = q_refs[r][0:rows, 0:HEAD]
-    for c in range(chunks):
+    for c, ref in enumerate(kv_refs):
         for b in range(per):
             at = slice((c * per + b) * tail, (c * per + b + 1) * tail)
-            tk_scr[at, :] = kv_refs[c][b, rows : rows + tail, 0:HEAD]
-            tv_scr[at, :] = kv_refs[c][b, rows : rows + tail, HEAD:]
-    n_text = chunks * per * tail
+            tk_scr[at, :] = ref[b, rows : rows + tail, 0:HEAD]
+            v_scr[at, 0:HEAD] = ref[b, rows : rows + tail, HEAD:]
+            v_at = (c * per + b) * rows + len(kv_refs) * per * tail
+            v_scr[v_at : v_at + rows, 0:HEAD] = ref[b, 0:rows, HEAD:]
+    v_scr[:, HEAD:] = jnp.ones((v_scr.shape[0], HEAD), jnp.bfloat16)
+    n_text = len(kv_refs) * per * tail
     marks = jnp.transpose(tk_scr[...].astype(jnp.float32))[0:1, :]
     marks = pltpu.roll(marks, n_text - texts, 1)
     lane = lax.broadcasted_iota(jnp.int32, (1, n_text), 1)
@@ -259,90 +261,83 @@
         return lax.dot_general(q, k, (((1,), (1,)), ((), ())), preferred_element_type=jnp.float32)
 
     def absorb(state, s, v):
-        top, total, acc = state
+        top, acc = state
         fresh = jnp.maximum(top, jnp.max(s, axis=-1, keepdims=True))
         p = jnp.exp(s - fresh)
         factor = jnp.exp(top - fresh)
-        total = total * factor + jnp.sum(p, axis=-1, keepdims=True)
         acc = acc * factor + jnp.dot(p.astype(jnp.bfloat16), v, preferred_element_type=jnp.float32)
-        return fresh, total, acc
+        return fresh, acc
 
     def tile(i, carry):
         at = pl.ds(pl.multiple_of(i * q_tile, q_tile), q_tile)
-        q = q_scr[at, :]
+        q = q_ref[at, :]
         state = (
             jnp.full((q_tile, 1), NEGATIVE, jnp.float32),
-            jnp.zeros((q_tile, 1), jnp.float32),
-            jnp.zeros((q_tile, HEAD), jnp.float32),
+            jnp.zeros((q_tile, 2 * HEAD), jnp.float32),
         )
         spans = [(ref, slice(b, b + k_blocks)) for ref in kv_refs for b in range(0, per, k_blocks)]
         ready = score(q, tk_scr[...]) + bias
-        value = tv_scr[...]
-        for ref, at_b in spans:
+        value = v_scr[0:n_text, :]
+        for n, (ref, at_b) in enumerate(spans):
             ahead = score(q, ref[at_b, 0:rows, 0:HEAD].reshape(k_blocks * rows, HEAD))
             state = absorb(state, ready, value)
-            ready, value = ahead, ref[at_b, 0:rows, HEAD:].reshape(k_blocks * rows, HEAD)
-        top, total, acc = absorb(state, ready, value)
-        top = jnp.broadcast_to(top, (q_tile, HEAD))
-        total = jnp.broadcast_to(total, (q_tile, HEAD))
-        if final:
-            top_in, total_in, acc_in = (ref[at, :] for ref in state_in)
-            high = jnp.maximum(top, top_in)
-            here, there = jnp.exp(top - high), jnp.exp(top_in - high)
-            acc = acc * here + acc_in * there
-            o_scr[at, :] = (acc / (total * here + total_in * there)).astype(jnp.bfloat16)
-        else:
-            outs[0][at, :] = top
-            outs[1][at, :] = total
-            outs[2][at, :] = acc
+            v_at = n_text + n * k_blocks * rows
+            ready, value = ahead, v_scr[v_at : v_at + k_blocks * rows, :]
+        top, acc = absorb(state, ready, value)
+        finish(at, jnp.broadcast_to(top, (q_tile, HEAD)), acc[:, HEAD:], acc[:, 0:HEAD])
         return carry
 
-    lax.fori_loop(0, tasks * rows // q_tile, tile, 0)
-    if final:
-        for r in range(tasks):
-            outs[r][...] = o_scr[r * rows : (r + 1) * rows, :]
-
-
-def attend(chunks, queries, state, rows, texts, final):
-    tasks = len(queries)
-    vmem = pl.BlockSpec(memory_space=pltpu.VMEM)
-    many = tasks * rows
-    n_text = sum(c.shape[0] for c in chunks) * (texts + PAD)
-    if final:
-        shapes = [jax.ShapeDtypeStruct((rows, HEAD), jnp.bfloat16)] * tasks
-    else:
-        shapes = [jax.ShapeDtypeStruct((many, HEAD), jnp.float32)] * 3
-    extra = [] if state is None else list(state)
-    return pl.pallas_call(
-        functools.partial(
-            attention_kernel, tasks=tasks, chunks=len(chunks), rows=rows, texts=texts, q_tile=2 * rows,
-            k_blocks=tasks // 2, final=final,
-        ),
-        out_shape=shapes,
-        in_specs=[vmem] * (len(chunks) + tasks + len(extra)),
-        out_specs=[vmem] * len(shapes),
-        scratch_shapes=[
-            pltpu.VMEM((many, HEAD), jnp.bfloat16),
-            pltpu.VMEM((many, HEAD), jnp.bfloat16),
-            pltpu.VMEM((n_text, HEAD), jnp.bfloat16),
-            pltpu.VMEM((n_text, HEAD), jnp.bfloat16),
-        ],
-        name="attention",
-    )(*chunks, *queries, *extra)
-
-
-def project_kernel(send_ref, valid_ref, w_ref, *refs, rounds):
-    ins, (mine_ref, other_ref, joined) = refs[:rounds], refs[rounds:]
+    lax.fori_loop(0, q_ref.shape[0] // q_tile, tile, 0)
+
+
+def attend_first_kernel(place_ref, own_ref, peer_ref, *refs, rows, texts, k_blocks):
+    *q_refs, top_ref, total_ref, acc_ref, q_out, tk_scr, v_scr = refs
+    here = lax.axis_index("seq") * lax.axis_size("tp") + lax.axis_index("tp")
+    for r, ref in enumerate(q_refs):
+        q_out[pl.ds(pl.multiple_of(place_ref[here, r] * rows, rows), rows), :] = ref[0:rows, 0:HEAD]
+
+    def finish(at, top, total, acc):
+        top_ref[at, :] = top
+        total_ref[at, :] = total
+        acc_ref[at, :] = acc
+
+    attend(q_out, (own_ref, peer_ref), tk_scr, v_scr, rows, texts, 2 * rows, k_blocks, finish)
+
+
+def attend_last_kernel(
+    kv_ref, kv2_ref, top_ref, total_ref, acc_ref, q_ref, out_ref, tk_scr, v_scr, *, rows, texts, k_blocks
+):
+    def finish(at, top, total, acc):
+        top_in, total_in = top_ref[at, :], total_ref[at, :]
+        high = jnp.maximum(top, top_in)
+        here, there = jnp.exp(top - high), jnp.exp(top_in - high)
+        acc = acc * here + acc_ref[at, :] * there
+        out_ref[at, :] = (acc / (total * here + total_in * there)).astype(jnp.bfloat16)
+
+    attend(q_ref, (kv_ref, kv2_ref), tk_scr, v_scr, rows, texts, 2 * rows, k_blocks, finish)
+
+
+def join_kernel(keep_ref, given_ref, *outs):
+    rows = outs[0].shape[0] // 2
+    for j, out in enumerate(outs):
+        out[0:rows, :] = keep_ref[j * rows : (j + 1) * rows, :]
+        out[rows:, :] = given_ref[j * rows : (j + 1) * rows, :]
+
+
+def project_kernel(heads_ref, valid_ref, w_ref, *refs):
+    *ins, mine_ref, other_ref, joined = refs
     share = mine_ref.shape[0]
     me = lax.axis_index("tp")
     here = lax.axis_index("seq") * lax.axis_size("tp") + me
 
-    for r in range(rounds):
-
-        @pl.when(valid_ref[here, r] == 1)
+    rows = joined.shape[0]
+    for j, ref in enumerate(ins):
+
+        @pl.when(valid_ref[here, j] == 1)
         def _():
-            at = pl.ds(pl.multiple_of(send_ref[here, r] * HEAD, HEAD), HEAD)
-            joined[:, at] = ins[r][...]
+            for h in range(2):
+                at = pl.ds(pl.multiple_of(heads_ref[here, 2 * j + h] * HEAD, HEAD), HEAD)
+                joined[:, at] = ref[h * rows : (h + 1) * rows, :]
 
     first = jnp.dot(joined[...], w_ref[...], preferred_element_type=jnp.float32).astype(jnp.bfloat16)
     low, high = first[:share], first[share:]
@@ -357,7 +352,8 @@
     texts = text_k.shape[0]
     heads = width // HEAD
     n_seq, n_tp = lax.axis_size("seq"), lax.axis_size("tp")
-    rounds, perms, send, valid, cross, flip = plan(n_seq, n_tp, heads)
+    perms, send, cross, flip, place, swap, perms_back, heads_back, valid = plan(n_seq, n_tp, heads)
+    rounds, backs = len(perms), len(perms_back)
     both = ("seq", "tp")
     full = rows + texts
     vmem = pl.BlockSpec(memory_space=pltpu.VMEM)
@@ -387,21 +383,58 @@
     )(*got)
     across = lax.ppermute(own, both, cross)
     peer = lax.ppermute(own, both, flip)
-    state = attend([own, peer], got, None, rows, texts, False)
+    many = rounds * rows
+    given = backs * rows
+    text_scratch = [
+        pltpu.VMEM((2 * rounds * (texts + PAD), HEAD), jnp.bfloat16),
+        pltpu.VMEM((2 * rounds * (rows + texts + PAD), 2 * HEAD), jnp.bfloat16),
+    ]
+    *state, queries = pl.pallas_call(
+        functools.partial(attend_first_kernel, rows=rows, texts=texts, k_blocks=rounds // 2),
+        out_shape=[jax.ShapeDtypeStruct((many, HEAD), jnp.float32)] * 3
+        + [jax.ShapeDtypeStruct((many, HEAD), jnp.bfloat16)],
+        in_specs=[smem] + [vmem] * (2 + rounds),
+        out_specs=[vmem] * 4,
+        scratch_shapes=text_scratch,
+        name="attention",
+    )(place, own, peer, *got)
     peer_across = lax.ppermute(across, both, flip)
-    outs = attend([across, peer_across], got, state, rows, texts, True)
-    back = [None] * rounds
-    for r in range(rounds):
-        back[r] = lax.ppermute(outs[r], both, [(d, s) for s, d in perms[r]])
+
+    def finish(part):
+        block = pl.BlockSpec((given, HEAD), lambda i: (part, 0))
+        whole_kv = pl.BlockSpec(own.shape, lambda i: (0, 0, 0))
+        return pl.pallas_call(
+            functools.partial(attend_last_kernel, rows=rows, texts=texts, k_blocks=rounds // 2),
+            out_shape=jax.ShapeDtypeStruct((given, HEAD), jnp.bfloat16),
+            grid=(1,),
+            in_specs=[whole_kv] * 2 + [block] * 4,
+            out_specs=pl.BlockSpec((given, HEAD), lambda i: (0, 0)),
+            scratch_shapes=text_scratch,
+            name="attention",
+        )(across, peer_across, *state, queries)
+
+    give = finish(0)
+    taken = lax.ppermute(give, both, swap)
+    keep = finish(1)
+    outs = pl.pallas_call(
+        join_kernel,
+        out_shape=[jax.ShapeDtypeStruct((2 * rows, HEAD), jnp.bfloat16)] * backs,
+        in_specs=[vmem] * 2,
+        out_specs=[vmem] * backs,
+        name="join",
+    )(keep, taken)
+    back = []
+    for o, p in zip(outs, perms_back):
+        back.append(lax.ppermute(o, both, p))
     share = rows // n_tp
     mine, other = pl.pallas_call(
-        functools.partial(project_kernel, rounds=rounds),
+        project_kernel,
         out_shape=[jax.ShapeDtypeStruct((share, w_out.shape[1]), jnp.bfloat16)] * 2,
-        in_specs=[smem] * 2 + [vmem] * (1 + rounds),
+        in_specs=[smem] * 2 + [vmem] * (1 + backs),
         out_specs=[vmem] * 2,
         scratch_shapes=[pltpu.VMEM((rows, width), jnp.bfloat16)],
         name="project",
-    )(send, valid, w_out, *back)
+    )(heads_back, valid, w_out, *back)
     theirs = lax.ppermute(other, "tp", [(0, 1), (1, 0)])
     return (mine.astype(jnp.float32) + theirs.astype(jnp.float32)).astype(jnp.bfloat16)
 

time: 290 us -> 282 us (0.972)
  starting transfers between devices: 192 us -> 146 us
  waiting for transfers between devices: 40.8 us -> 75.7 us
    ppermute x8, starting transfers between devices: 117 us -> 90.8 us  [body(): got.append(lax.ppermute(b, both, perms[r]))]
    ppermute x8 -> x5, starting transfers between devices: 59.5 us -> 36.6 us  [the longest x4 24.7 us: body(): back.append(lax.ppermute(o, both, p))]
    ppermute x8 -> x5, waiting for transfers between devices: 1.56 us -> 21.9 us  [the longest x4 18.8 us: body(): back.append(lax.ppermute(o, both, p))]
    ppermute x8, waiting for transfers between devices: 20.2 us -> 36.1 us  [body(): got.append(lax.ppermute(b, both, perms[r]))]
    ppermute x1, starting transfers between devices: 1.94 us -> 5.36 us  [body(): across = lax.ppermute(own, both, cross)]
    pallas_call x3 -> x5, Pallas kernels: 38.1 us -> 40.3 us  [the longest x2 18.1 us: finish(): pl.pallas_call(functools.partial(attend_last_kernel, rows=rows, texts=tex...]
  transfers between devices with their start and end apart: 20 -> 17, of which waited for: 6 -> 7; matrix products, arithmetic and copies ran while one was open for 0% -> 0% of each run, Pallas kernels for 7% -> 10%
where the time goes in v1:
time: 282 us; the launch traced here: 281 us
  starting transfers between devices  146 us (52%)
  waiting for transfers between devices  75.7 us (27%)
  Pallas kernels  51.4 us (18%)
  local copies, waits for them, and re-layouts  4.71 us (2%)
    ppermute x8, starting transfers between devices, body(): got.append(lax.ppermute(b, both, perms[r]))  90.8 us
    ppermute x8, waiting for transfers between devices, body(): got.append(lax.ppermute(b, both, perms[r]))  36.1 us
    ppermute x4, starting transfers between devices, body(): back.append(lax.ppermute(o, both, p))  24.7 us
    ppermute x4, waiting for transfers between devices, body(): back.append(lax.ppermute(o, both, p))  18.8 us
    pallas_call x2, Pallas kernels, finish(): pl.pallas_call(functools.partial(attend_last_kernel, rows=rows, texts=tex...  18.1 us
    ppermute x1, waiting for transfers between devices, body(): across = lax.ppermute(own, both, cross)  15.3 us
    pallas_call x1, Pallas kernels, body(): pl.pallas_call(functools.partial(attend_first_kernel, rows=rows, texts=te...  15.3 us
    ppermute x1, starting transfers between devices, body(): taken = lax.ppermute(give, both, swap)  11.8 us
  transfers between devices with their start and end apart: 17, of which 7 were waited for; matrix products, arithmetic and copies ran while one was open for 0% of the time, Pallas kernels for 10%

profile of v1, /device:TPU:37, one launch (start us, length us, event | category | flops | bytes accessed | tf_op | source)
XLA Modules:
  0.0 281.3 jit_solution(13261693809772742983)
XLA Ops:
  0.7 4.3 %prep.3 = (bf16[264,384]{1,0:T(8,128)(2,1)}, bf16[264,384]{1,0:T(8,128)(2,1)}, bf16[264,384]{1,0:T(8,128)(2,1)}, bf16[264,384]{1,0:T(8,128)(2,1)}) custom-call(s32[64,8]{1,0:T(8,128)} %constant.16.clone.send_ref, s32[8]{0:T(128)} %mask_ref.3, s32[1]{0:T(128)S(6)} %copy.19.slab_ref, bf16[256,768]{1,0:T(8,128)(2,1)} %q_ref.3, bf16[256,768]{1,0:T(8,128)(2,1)} %k_ref.3, ...), custom_call_target="tpu_custom_call" | custom-call | tf_op jit(solution)/shard_map/prep/pallas_call | solution.py:365
  5.0 1.3 collective-permute-start.4
  6.3 28.2 %collective-permute-start.5 = (bf16[264,384]{1,0:T(8,128)(2,1)}, bf16[264,384]{1,0:T(8,128)(2,1)S(1)}, u32[]{:S(2)}, u32[]{:S(2)}) collective-permute-start(bf16[264,384]{1,0:T(8,128)(2,1)} %get-tuple-element.28), channel_id=1, source_target_pairs={{0,51},{1,54},{2,20},{3,17},{4,21},{5,16},{7,55},{9,10},{10,3},{11... | collective-permute-start | bytes 608264 | tf_op jit(solution)/shard_map/ppermute | solution.py:376
  34.4 8.6 %collective-permute-start.6 = (bf16[264,384]{1,0:T(8,128)(2,1)}, bf16[264,384]{1,0:T(8,128)(2,1)S(1)}, u32[]{:S(2)}, u32[]{:S(2)}) collective-permute-start(bf16[264,384]{1,0:T(8,128)(2,1)} %get-tuple-element.29), channel_id=1, source_target_pairs={{0,27},{1,10},{2,50},{3,61},{4,51},{5,60},{6,26},{8,21},{9,54},{10... | collective-permute-start | bytes 608264 | tf_op jit(solution)/shard_map/ppermute | solution.py:376
  43.1 4.3 %collective-permute-start.7 = (bf16[264,384]{1,0:T(8,128)(2,1)}, bf16[264,384]{1,0:T(8,128)(2,1)S(1)}, u32[]{:S(2)}, u32[]{:S(2)}) collective-permute-start(bf16[264,384]{1,0:T(8,128)(2,1)} %get-tuple-element.30), channel_id=1, source_target_pairs={{0,45},{1,16},{2,44},{3,11},{5,54},{7,61},{8,27},{10,26},{11,55},{... | collective-permute-start | bytes 608264 | tf_op jit(solution)/shard_map/ppermute | solution.py:376
  47.4 4.2 %prep.2 = (bf16[264,384]{1,0:T(8,128)(2,1)}, bf16[264,384]{1,0:T(8,128)(2,1)}, bf16[264,384]{1,0:T(8,128)(2,1)}, bf16[264,384]{1,0:T(8,128)(2,1)}) custom-call(s32[64,8]{1,0:T(8,128)} %constant.16.clone.send_ref, s32[8]{0:T(128)} %mask_ref.3, s32[1]{0:T(128)S(6)} %copy.19.slab_ref, bf16[256,768]{1,0:T(8,128)(2,1)} %q_ref.3, bf16[256,768]{1,0:T(8,128)(2,1)} %k_ref.3, ...), custom_call_target="tpu_custom_call" | custom-call | tf_op jit(solution)/shard_map/prep/pallas_call | solution.py:365
  51.6 13.9 %collective-permute-start = (bf16[264,384]{1,0:T(8,128)(2,1)}, bf16[264,384]{1,0:T(8,128)(2,1)S(1)}, u32[]{:S(2)}, u32[]{:S(2)}) collective-permute-start(bf16[264,384]{1,0:T(8,128)(2,1)} %get-tuple-element.23), channel_id=1, source_target_pairs={{1,38},{3,39},{5,37},{6,44},{7,32},{8,51},{9,33},{10,50},{12,45},{... | collective-permute-start | bytes 608264 | tf_op jit(solution)/shard_map/ppermute | solution.py:376
  65.5 0.0 collective-permute-done.4.refs_4_
  65.5 1.3 collective-permute-start.1
  66.8 6.3 %collective-permute-done.5.refs_5_ = bf16[264,384]{1,0:T(8,128)(2,1)S(1)} collective-permute-done((bf16[264,384]{1,0:T(8,128)(2,1)}, bf16[264,384]{1,0:T(8,128)(2,1)S(1)}, u32[]{:S(2)}, u32[]{:S(2)}) %collective-permute-start.5) | collective-permute-done | bytes 202784 | tf_op jit(solution)/shard_map/ppermute | solution.py:376
  73.2 1.9 collective-permute-start.2
  75.1 17.5 %collective-permute-done.6.refs_6_ = bf16[264,384]{1,0:T(8,128)(2,1)S(1)} collective-permute-done((bf16[264,384]{1,0:T(8,128)(2,1)}, bf16[264,384]{1,0:T(8,128)(2,1)S(1)}, u32[]{:S(2)}, u32[]{:S(2)}) %collective-permute-start.6) | collective-permute-done | bytes 202784 | tf_op jit(solution)/shard_map/ppermute | solution.py:376
  92.6 31.3 %collective-permute-start.3 = (bf16[264,384]{1,0:T(8,128)(2,1)}, bf16[264,384]{1,0:T(8,128)(2,1)S(1)}, u32[]{:S(2)}, u32[]{:S(2)}) collective-permute-start(bf16[264,384]{1,0:T(8,128)(2,1)} %get-tuple-element.26), channel_id=1, source_target_pairs={{0,1},{1,60},{2,0},{4,6},{6,7},{7,17},{8,2},{9,16},{11,11},{13,10}... | collective-permute-start | bytes 608264 | tf_op jit(solution)/shard_map/ppermute | solution.py:376
  123.9 0.0 collective-permute-done.7.refs_7_
  123.9 0.0 collective-permute-done.refs_0_
  124.0 0.0 collective-permute-done.1.refs_1_
  124.0 0.0 collective-permute-done.2.refs_2_
  124.0 12.3 %collective-permute-done.3.refs_3_ = bf16[264,384]{1,0:T(8,128)(2,1)S(1)} collective-permute-done((bf16[264,384]{1,0:T(8,128)(2,1)}, bf16[264,384]{1,0:T(8,128)(2,1)S(1)}, u32[]{:S(2)}, u32[]{:S(2)}) %collective-permute-start.3) | collective-permute-done | bytes 202784 | tf_op jit(solution)/shard_map/ppermute | solution.py:376
  136.3 0.7 copy-done.10
  137.0 2.6 pack.1.own_ref
  139.6 5.4 %collective-permute-start.8 = (bf16[8,272,256]{2,1,0:T(8,128)(2,1)}, bf16[8,272,256]{2,1,0:T(8,128)(2,1)S(1)}, u32[]{:S(2)}, u32[]{:S(2)}) collective-permute-start(bf16[8,272,256]{2,1,0:T(8,128)(2,1)} %pack.1.own_ref), channel_id=1, source_target_pairs={{0,2},{2,0},{1,3},{3,1},{4,6},{6,4},{5,7},{7,5},{10,12},{12,10},{1... | collective-permute-start | bytes 3342344 | tf_op jit(solution)/shard_map/ppermute | solution.py:384
  144.9 6.5 %collective-permute-start.10 = (bf16[8,272,256]{2,1,0:T(8,128)(2,1)}, bf16[8,272,256]{2,1,0:T(8,128)(2,1)S(1)}, u32[]{:S(2)}, u32[]{:S(2)}) collective-permute-start(bf16[8,272,256]{2,1,0:T(8,128)(2,1)} %pack.1.own_ref), channel_id=1, source_target_pairs={{0,1},{2,3},{1,0},{3,2},{4,5},{6,7},{5,4},{7,6},{10,11},{12,13},{1... | collective-permute-start | bytes 3342344 | tf_op jit(solution)/shard_map/ppermute | solution.py:385
  151.4 15.3 %collective-permute-done.8.kv_ref = bf16[8,272,256]{2,1,0:T(8,128)(2,1)S(1)} collective-permute-done((bf16[8,272,256]{2,1,0:T(8,128)(2,1)}, bf16[8,272,256]{2,1,0:T(8,128)(2,1)S(1)}, u32[]{:S(2)}, u32[]{:S(2)}) %collective-permute-start.8) | collective-permute-done | bytes 1114144 | tf_op jit(solution)/shard_map/ppermute | solution.py:384
  166.8 6.9 %collective-permute-start.9 = (bf16[8,272,256]{2,1,0:T(8,128)(2,1)S(1)}, bf16[8,272,256]{2,1,0:T(8,128)(2,1)S(1)}, u32[]{:S(2)}, u32[]{:S(2)}) collective-permute-start(bf16[8,272,256]{2,1,0:T(8,128)(2,1)S(1)} %collective-permute-done.8.kv_ref), channel_id=1, source_target_pairs={{0,1},{2,3},{1,0},{3,2},{4,5},{6,7},{5,4},{7,6},{10,11},{12,13},{1... | collective-permute-start | bytes 3342344 | tf_op jit(solution)/shard_map/ppermute | solution.py:401
  173.7 0.0 collective-permute-done.10.peer_ref
  173.7 1.0 copy-done.2
  174.7 15.3 %attention.3 = (f32[2048,128]{1,0:T(8,128)}, f32[2048,128]{1,0:T(8,128)}, f32[2048,128]{1,0:T(8,128)}, bf16[2048,128]{1,0:T(8,128)(2,1)}) custom-call(s32[64,8]{1,0:T(8,128)} %constant.21.clone.place_ref, bf16[8,272,256]{2,1,0:T(8,128)(2,1)} %pack.1.own_ref, bf16[8,272,256]{2,1,0:T(8,128)(2,1)} %copy-done.2, bf16[264,384]{1,0:T(8,128)(2,1)} %copy-done.7, ...), custom_call_target="tpu_custom_call" | custom-call | tf_op jit(solution)/shard_map/attention/pallas_call | solution.py:392
  190.0 1.0 copy-done.1
  191.0 9.0 %attention.5 = bf16[1024,128]{1,0:T(8,128)(2,1)} custom-call(bf16[8,272,256]{2,1,0:T(8,128)(2,1)} %copy-done, bf16[8,272,256]{2,1,0:T(8,128)(2,1)} %copy-done.1, f32[2048,128]{1,0:T(8,128)} %get-tuple-element.31.top_ref, f32[2048,128]{1,0:T(8,128)} %get-tuple-element.32.total_ref, f32[2048,128]{1,0:T(8,128)} %get-tuple-element.33.acc_ref, ...), custom_call_target="tpu_custom_call" | custom-call | tf_op jit(solution)/shard_map/attention/pallas_call | solution.py:406
  200.0 11.8 %collective-permute-start.11 = (bf16[1024,128]{1,0:T(8,128)(2,1)}, bf16[1024,128]{1,0:T(8,128)(2,1)S(1)}, u32[]{:S(2)}, u32[]{:S(2)}) collective-permute-start(bf16[1024,128]{1,0:T(8,128)(2,1)} %attention.5), channel_id=1, source_target_pairs={{0,4},{1,5},{2,6},{3,7},{4,0},{5,1},{6,2},{7,3},{10,16},{11,17},{1... | collective-permute-start | bytes 786440 | tf_op jit(solution)/shard_map/ppermute | solution.py:417
  211.9 9.0 %attention.4.keep_ref = bf16[1024,128]{1,0:T(8,128)(2,1)} custom-call(bf16[8,272,256]{2,1,0:T(8,128)(2,1)} %copy-done, bf16[8,272,256]{2,1,0:T(8,128)(2,1)} %copy-done.1, f32[2048,128]{1,0:T(8,128)} %get-tuple-element.31.top_ref, f32[2048,128]{1,0:T(8,128)} %get-tuple-element.32.total_ref, f32[2048,128]{1,0:T(8,128)} %get-tuple-element.33.acc_ref, ...), custom_call_target="tpu_custom_call" | custom-call | tf_op jit(solution)/shard_map/attention/pallas_call | solution.py:406
  220.9 3.0 %collective-permute-done.11.given_ref = bf16[1024,128]{1,0:T(8,128)(2,1)S(1)} collective-permute-done((bf16[1024,128]{1,0:T(8,128)(2,1)}, bf16[1024,128]{1,0:T(8,128)(2,1)S(1)}, u32[]{:S(2)}, u32[]{:S(2)}) %collective-permute-start.11) | collective-permute-done | bytes 262176 | tf_op jit(solution)/shard_map/ppermute | solution.py:417
  223.9 0.7 copy-done.11
  224.6 1.8 join.1
  226.5 7.5 %collective-permute-start.12 = (bf16[512,128]{1,0:T(8,128)(2,1)}, bf16[512,128]{1,0:T(8,128)(2,1)S(1)}, u32[]{:S(2)}, u32[]{:S(2)}) collective-permute-start(bf16[512,128]{1,0:T(8,128)(2,1)} %get-tuple-element.35), channel_id=1, source_target_pairs={{16,1},{50,2},{39,3},{51,4},{54,5},{55,7},{27,8},{33,9},{26,10},{3... | collective-permute-start | bytes 393224 | tf_op jit(solution)/shard_map/ppermute | solution.py:428
  233.9 8.7 %collective-permute-start.13 = (bf16[512,128]{1,0:T(8,128)(2,1)}, bf16[512,128]{1,0:T(8,128)(2,1)S(1)}, u32[]{:S(2)}, u32[]{:S(2)}) collective-permute-start(bf16[512,128]{1,0:T(8,128)(2,1)} %get-tuple-element.36), channel_id=1, source_target_pairs={{21,0},{38,1},{4,2},{17,3},{33,5},{50,6},{32,7},{51,8},{16,9},{2,1... | collective-permute-start | bytes 393224 | tf_op jit(solution)/shard_map/ppermute | solution.py:428
  242.6 1.3 collective-permute-start.14
  244.0 7.3 %collective-permute-start.15 = (bf16[512,128]{1,0:T(8,128)(2,1)}, bf16[512,128]{1,0:T(8,128)(2,1)S(1)}, u32[]{:S(2)}, u32[]{:S(2)}) collective-permute-start(bf16[512,128]{1,0:T(8,128)(2,1)} %get-tuple-element.38), channel_id=1, source_target_pairs={{51,0},{54,1},{21,4},{20,6},{17,7},{2,8},{60,9},{3,10},{61,11},{27... | collective-permute-start | bytes 393224 | tf_op jit(solution)/shard_map/ppermute | solution.py:428
  251.2 18.8 %collective-permute-done.13.refs_1_ = bf16[512,128]{1,0:T(8,128)(2,1)S(1)} collective-permute-done((bf16[512,128]{1,0:T(8,128)(2,1)}, bf16[512,128]{1,0:T(8,128)(2,1)S(1)}, u32[]{:S(2)}, u32[]{:S(2)}) %collective-permute-start.13) | collective-permute-done | bytes 131104 | tf_op jit(solution)/shard_map/ppermute | solution.py:428
  270.1 0.0 collective-permute-done.14.refs_2_
  270.1 0.0 collective-permute-done.15.refs_3_
  270.1 0.6 copy-done.13
  270.7 0.1 copy-done.14
  270.8 0.6 copy-done.15
  271.4 5.1 %project.1 = (bf16[128,3072]{1,0:T(8,128)(2,1)}, bf16[128,3072]{1,0:T(8,128)(2,1)}) custom-call(s32[64,8]{1,0:T(8,128)} %constant.22.clone.heads_ref, s32[64,4]{1,0:T(8,128)} %constant.23.clone.valid_ref, bf16[768,3072]{1,0:T(8,128)(2,1)} %w_ref.1, bf16[512,128]{1,0:T(8,128)(2,1)} %copy-done.12, bf16[512,128]{1,0:T(8,128)(2,1)} %copy-done.13, ...), custom_call_target="tpu_custom_call" | custom-call | tf_op jit(solution)/shard_map/project/pallas_call | solution.py:430
  276.6 0.2 collective-permute-start.16
  276.7 2.3 collective-permute-done.16
  279.1 2.2 add_convert_fusion
  (27 shorter events, 0.1 us)
Async XLA Ops:
  5.0 60.5 %collective-permute-start.4 = (bf16[264,384]{1,0:T(8,128)(2,1)}, bf16[264,384]{1,0:T(8,128)(2,1)S(1)}, u32[]{:S(2)}, u32[]{:S(2)}) collective-permute-start(bf16[264,384]{1,0:T(8,128)(2,1)} %get-tuple-element.27), channel_id=1, source_target_pairs={{0,21},{2,26},{3,55},{4,27},{5,33},{6,20},{8,45},{9,60},{11,36},{1... | collective-permute-start | bytes 608264 | tf_op jit(solution)/shard_map/ppermute | solution.py:376
  6.3 66.9 %collective-permute-start.5 = (bf16[264,384]{1,0:T(8,128)(2,1)}, bf16[264,384]{1,0:T(8,128)(2,1)S(1)}, u32[]{:S(2)}, u32[]{:S(2)}) collective-permute-start(bf16[264,384]{1,0:T(8,128)(2,1)} %get-tuple-element.28), channel_id=1, source_target_pairs={{0,51},{1,54},{2,20},{3,17},{4,21},{5,16},{7,55},{9,10},{10,3},{11... | collective-permute-start | bytes 608264 | tf_op jit(solution)/shard_map/ppermute | solution.py:376
  34.4 58.2 %collective-permute-start.6 = (bf16[264,384]{1,0:T(8,128)(2,1)}, bf16[264,384]{1,0:T(8,128)(2,1)S(1)}, u32[]{:S(2)}, u32[]{:S(2)}) collective-permute-start(bf16[264,384]{1,0:T(8,128)(2,1)} %get-tuple-element.29), channel_id=1, source_target_pairs={{0,27},{1,10},{2,50},{3,61},{4,51},{5,60},{6,26},{8,21},{9,54},{10... | collective-permute-start | bytes 608264 | tf_op jit(solution)/shard_map/ppermute | solution.py:376
  43.1 80.8 %collective-permute-start.7 = (bf16[264,384]{1,0:T(8,128)(2,1)}, bf16[264,384]{1,0:T(8,128)(2,1)S(1)}, u32[]{:S(2)}, u32[]{:S(2)}) collective-permute-start(bf16[264,384]{1,0:T(8,128)(2,1)} %get-tuple-element.30), channel_id=1, source_target_pairs={{0,45},{1,16},{2,44},{3,11},{5,54},{7,61},{8,27},{10,26},{11,55},{... | collective-permute-start | bytes 608264 | tf_op jit(solution)/shard_map/ppermute | solution.py:376
  51.6 72.3 %collective-permute-start = (bf16[264,384]{1,0:T(8,128)(2,1)}, bf16[264,384]{1,0:T(8,128)(2,1)S(1)}, u32[]{:S(2)}, u32[]{:S(2)}) collective-permute-start(bf16[264,384]{1,0:T(8,128)(2,1)} %get-tuple-element.23), channel_id=1, source_target_pairs={{1,38},{3,39},{5,37},{6,44},{7,32},{8,51},{9,33},{10,50},{12,45},{... | collective-permute-start | bytes 608264 | tf_op jit(solution)/shard_map/ppermute | solution.py:376
  65.5 70.8 %copy-start.3 = (bf16[264,384]{1,0:T(8,128)(2,1)}, bf16[264,384]{1,0:T(8,128)(2,1)S(1)}, u32[]{:S(2)}) copy-start(bf16[264,384]{1,0:T(8,128)(2,1)S(1)} %collective-permute-done.4.refs_4_) | copy-start | bytes 608260
  65.5 58.4 %collective-permute-start.1 = (bf16[264,384]{1,0:T(8,128)(2,1)}, bf16[264,384]{1,0:T(8,128)(2,1)S(1)}, u32[]{:S(2)}, u32[]{:S(2)}) collective-permute-start(bf16[264,384]{1,0:T(8,128)(2,1)} %get-tuple-element.24), channel_id=1, source_target_pairs={{0,5},{2,4},{4,2},{5,10},{6,3},{7,11},{8,6},{10,7},{11,17},{13,16}... | collective-permute-start | bytes 608264 | tf_op jit(solution)/shard_map/ppermute | solution.py:376
  73.2 63.1 %copy-start.4 = (bf16[264,384]{1,0:T(8,128)(2,1)}, bf16[264,384]{1,0:T(8,128)(2,1)S(1)}, u32[]{:S(2)}) copy-start(bf16[264,384]{1,0:T(8,128)(2,1)S(1)} %collective-permute-done.5.refs_5_) | copy-start | bytes 608260
  73.2 50.8 %collective-permute-start.2 = (bf16[264,384]{1,0:T(8,128)(2,1)}, bf16[264,384]{1,0:T(8,128)(2,1)S(1)}, u32[]{:S(2)}, u32[]{:S(2)}) collective-permute-start(bf16[264,384]{1,0:T(8,128)(2,1)} %get-tuple-element.25), channel_id=1, source_target_pairs={{1,34},{3,35},{4,45},{6,50},{7,36},{9,37},{10,44},{11,32},{12,51},... | collective-permute-start | bytes 608264 | tf_op jit(solution)/shard_map/ppermute | solution.py:376
  92.6 43.7 %copy-start.5 = (bf16[264,384]{1,0:T(8,128)(2,1)}, bf16[264,384]{1,0:T(8,128)(2,1)S(1)}, u32[]{:S(2)}) copy-start(bf16[264,384]{1,0:T(8,128)(2,1)S(1)} %collective-permute-done.6.refs_6_) | copy-start | bytes 608260
  92.6 43.7 %collective-permute-start.3 = (bf16[264,384]{1,0:T(8,128)(2,1)}, bf16[264,384]{1,0:T(8,128)(2,1)S(1)}, u32[]{:S(2)}, u32[]{:S(2)}) collective-permute-start(bf16[264,384]{1,0:T(8,128)(2,1)} %get-tuple-element.26), channel_id=1, source_target_pairs={{0,1},{1,60},{2,0},{4,6},{6,7},{7,17},{8,2},{9,16},{11,11},{13,10}... | collective-permute-start | bytes 608264 | tf_op jit(solution)/shard_map/ppermute | solution.py:376
  123.9 12.4 %copy-start.6 = (bf16[264,384]{1,0:T(8,128)(2,1)}, bf16[264,384]{1,0:T(8,128)(2,1)S(1)}, u32[]{:S(2)}) copy-start(bf16[264,384]{1,0:T(8,128)(2,1)S(1)} %collective-permute-done.7.refs_7_) | copy-start | bytes 608260
  123.9 12.4 %copy-start.7 = (bf16[264,384]{1,0:T(8,128)(2,1)}, bf16[264,384]{1,0:T(8,128)(2,1)S(1)}, u32[]{:S(2)}) copy-start(bf16[264,384]{1,0:T(8,128)(2,1)S(1)} %collective-permute-done.refs_0_) | copy-start | bytes 608260
  124.0 12.4 %copy-start.8 = (bf16[264,384]{1,0:T(8,128)(2,1)}, bf16[264,384]{1,0:T(8,128)(2,1)S(1)}, u32[]{:S(2)}) copy-start(bf16[264,384]{1,0:T(8,128)(2,1)S(1)} %collective-permute-done.1.refs_1_) | copy-start | bytes 608260
  124.0 12.3 %copy-start.9 = (bf16[264,384]{1,0:T(8,128)(2,1)}, bf16[264,384]{1,0:T(8,128)(2,1)S(1)}, u32[]{:S(2)}) copy-start(bf16[264,384]{1,0:T(8,128)(2,1)S(1)} %collective-permute-done.2.refs_2_) | copy-start | bytes 608260
  136.3 0.7 copy-start.10
  139.6 27.2 %collective-permute-start.8 = (bf16[8,272,256]{2,1,0:T(8,128)(2,1)}, bf16[8,272,256]{2,1,0:T(8,128)(2,1)S(1)}, u32[]{:S(2)}, u32[]{:S(2)}) collective-permute-start(bf16[8,272,256]{2,1,0:T(8,128)(2,1)} %pack.1.own_ref), channel_id=1, source_target_pairs={{0,2},{2,0},{1,3},{3,1},{4,6},{6,4},{5,7},{7,5},{10,12},{12,10},{1... | collective-permute-start | bytes 3342344 | tf_op jit(solution)/shard_map/ppermute | solution.py:384
  144.9 28.7 %collective-permute-start.10 = (bf16[8,272,256]{2,1,0:T(8,128)(2,1)}, bf16[8,272,256]{2,1,0:T(8,128)(2,1)S(1)}, u32[]{:S(2)}, u32[]{:S(2)}) collective-permute-start(bf16[8,272,256]{2,1,0:T(8,128)(2,1)} %pack.1.own_ref), channel_id=1, source_target_pairs={{0,1},{2,3},{1,0},{3,2},{4,5},{6,7},{5,4},{7,6},{10,11},{12,13},{1... | collective-permute-start | bytes 3342344 | tf_op jit(solution)/shard_map/ppermute | solution.py:385
  166.8 23.2 %copy-start = (bf16[8,272,256]{2,1,0:T(8,128)(2,1)}, bf16[8,272,256]{2,1,0:T(8,128)(2,1)S(1)}, u32[]{:S(2)}) copy-start(bf16[8,272,256]{2,1,0:T(8,128)(2,1)S(1)} %collective-permute-done.8.kv_ref) | copy-start | bytes 3342340
  166.8 23.2 %collective-permute-start.9 = (bf16[8,272,256]{2,1,0:T(8,128)(2,1)S(1)}, bf16[8,272,256]{2,1,0:T(8,128)(2,1)S(1)}, u32[]{:S(2)}, u32[]{:S(2)}) collective-permute-start(bf16[8,272,256]{2,1,0:T(8,128)(2,1)S(1)} %collective-permute-done.8.kv_ref), channel_id=1, source_target_pairs={{0,1},{2,3},{1,0},{3,2},{4,5},{6,7},{5,4},{7,6},{10,11},{12,13},{1... | collective-permute-start | bytes 3342344 | tf_op jit(solution)/shard_map/ppermute | solution.py:401
  173.7 1.0 copy-start.2
  190.0 1.0 copy-start.1
  200.0 23.9 %collective-permute-start.11 = (bf16[1024,128]{1,0:T(8,128)(2,1)}, bf16[1024,128]{1,0:T(8,128)(2,1)S(1)}, u32[]{:S(2)}, u32[]{:S(2)}) collective-permute-start(bf16[1024,128]{1,0:T(8,128)(2,1)} %attention.5), channel_id=1, source_target_pairs={{0,4},{1,5},{2,6},{3,7},{4,0},{5,1},{6,2},{7,3},{10,16},{11,17},{1... | collective-permute-start | bytes 786440 | tf_op jit(solution)/shard_map/ppermute | solution.py:417
  223.9 0.7 copy-start.11
  226.5 24.8 %collective-permute-start.12 = (bf16[512,128]{1,0:T(8,128)(2,1)}, bf16[512,128]{1,0:T(8,128)(2,1)S(1)}, u32[]{:S(2)}, u32[]{:S(2)}) collective-permute-start(bf16[512,128]{1,0:T(8,128)(2,1)} %get-tuple-element.35), channel_id=1, source_target_pairs={{16,1},{50,2},{39,3},{51,4},{54,5},{55,7},{27,8},{33,9},{26,10},{3... | collective-permute-start | bytes 393224 | tf_op jit(solution)/shard_map/ppermute | solution.py:428
  233.9 36.2 %collective-permute-start.13 = (bf16[512,128]{1,0:T(8,128)(2,1)}, bf16[512,128]{1,0:T(8,128)(2,1)S(1)}, u32[]{:S(2)}, u32[]{:S(2)}) collective-permute-start(bf16[512,128]{1,0:T(8,128)(2,1)} %get-tuple-element.36), channel_id=1, source_target_pairs={{21,0},{38,1},{4,2},{17,3},{33,5},{50,6},{32,7},{51,8},{16,9},{2,1... | collective-permute-start | bytes 393224 | tf_op jit(solution)/shard_map/ppermute | solution.py:428
  242.6 27.5 %collective-permute-start.14 = (bf16[512,128]{1,0:T(8,128)(2,1)}, bf16[512,128]{1,0:T(8,128)(2,1)S(1)}, u32[]{:S(2)}, u32[]{:S(2)}) collective-permute-start(bf16[512,128]{1,0:T(8,128)(2,1)} %get-tuple-element.37), channel_id=1, source_target_pairs={{5,0},{20,2},{55,3},{2,4},{16,5},{3,6},{50,10},{17,11},{51,12},{33... | collective-permute-start | bytes 393224 | tf_op jit(solution)/shard_map/ppermute | solution.py:428
  244.0 26.1 %collective-permute-start.15 = (bf16[512,128]{1,0:T(8,128)(2,1)}, bf16[512,128]{1,0:T(8,128)(2,1)S(1)}, u32[]{:S(2)}, u32[]{:S(2)}) collective-permute-start(bf16[512,128]{1,0:T(8,128)(2,1)} %get-tuple-element.38), channel_id=1, source_target_pairs={{51,0},{54,1},{21,4},{20,6},{17,7},{2,8},{60,9},{3,10},{61,11},{27... | collective-permute-start | bytes 393224 | tf_op jit(solution)/shard_map/ppermute | solution.py:428
  251.2 18.9 %copy-start.12 = (bf16[512,128]{1,0:T(8,128)(2,1)}, bf16[512,128]{1,0:T(8,128)(2,1)S(1)}, u32[]{:S(2)}) copy-start(bf16[512,128]{1,0:T(8,128)(2,1)S(1)} %collective-permute-done.12.refs_0_) | copy-start | bytes 393220
  270.1 0.6 copy-start.13
  270.1 0.7 copy-start.14
  270.8 0.6 copy-start.15
  276.6 2.5 collective-permute-start.16
